TPU v7x, 256 devices: a whole 4x4x8 slice. The times are simulated.
256 devices in a mesh: clip: 4 (over z_lo), vid: 8 (over y, core), aud: 8 (over x, z_hi).
Axes of the slice: x: 4, y: 4, z: 8 (z_hi: 2, z_lo: 4; z = z_hi * 4 + z_lo), core: 2. Of those that a mesh axis runs over, the one named last changes fastest.
Arguments:
- video_tokens: bfloat16 [4, 1024, 2048], P('clip', 'vid'), may hold values from -6 to 6
- audio_tokens: bfloat16 [4, 1024, 2048], P('clip', 'vid'), may hold values from -6 to 6
- qkv_video: bfloat16 [2048, 16, 384], P(None, 'aud'), may hold values from -0.125 to 0.125
- out_video: bfloat16 [16, 128, 2048], P('aud'), may hold values from -0.125 to 0.125
- qkv_audio: bfloat16 [2048, 16, 384], P(None, 'aud'), may hold values from -0.125 to 0.125
- out_audio: bfloat16 [16, 128, 2048], P('aud'), may hold values from -0.125 to 0.125
- gain_video: float32 [2048], replicated, may hold values from 0.5 to 1.5
- gain_audio: float32 [2048], replicated, may hold values from 0.5 to 1.5
- time_from: float32 [65, 2048], replicated, may hold values from -1.8 to 1.8
- time_to: float32 [65, 2048], replicated, may hold values from -1.8 to 1.8
- time_steps: int32 [4, 2], P('clip'), may hold values from 0 to 64, as said below
- windows: int32 [4, 2], P('clip'), may hold values from 32 to 128
- intersection: int32 [4, 32, 2], P('clip'), may hold values from 0 to 32, as said below
Outputs:
- d_video: bfloat16 [4, 1024, 2048], P('clip', 'vid')
- d_audio: bfloat16 [4, 1024, 2048], P('clip', 'vid')
- grad_qkv_video: float32 [2048, 16, 384], P(('clip', 'vid'), 'aud')
- grad_out_video: float32 [16, 128, 2048], P('aud', None, ('clip', 'vid'))
- grad_qkv_audio: float32 [2048, 16, 384], P(('clip', 'vid'), 'aud')
- grad_out_audio: float32 [16, 128, 2048], P('aud', None, ('clip', 'vid'))
Inputs may be any that keep to these rules, and one draw needn't show every extreme that they name: `time_steps`: column 1 (m) is 1 or more and 2 * m <= column 0 (t) <= 64. `intersection`: entry b holds (lo, hi) with lo < hi, max(b * 32 - 128, 0) <= lo * 32 <= b * 32 and (hi - lo) * 32 <= 160.
All inputs are finite; a program needn't handle non-finite values.
Results may differ from a plain program's by a relative error of at most 0.029.
Values may be sent and summed in bfloat16 or wider, within the bound.
A program may use at most 128 MiB of HBM per device.

v0:
```python
import jax
import jax.numpy as jnp
from jax import lax
from jax.sharding import PartitionSpec as P

BLK = 32
TGRID = 64
STEPS = 2


EPSILON = 1e-06
PRECISE = lax.Precision.HIGHEST


def padded(block, sides, width):
    for axis, dim in sides:
        count = lax.axis_size(axis)
        forward = [(i, i + 1) for i in range(count - 1)]
        backward = [(target, source) for source, target in forward]
        low = lax.ppermute(
            lax.slice_in_dim(block, block.shape[dim] - width, None, axis=dim), axis, forward
        )
        high = lax.ppermute(lax.slice_in_dim(block, 0, width, axis=dim), axis, backward)
        block = jnp.concatenate([low, block, high], axis=dim)
    return block


def shifted_2(block, axis, distance):
    devices = range(lax.axis_size(axis))
    route = [(i - distance, i) for i in devices if i - distance in devices]
    return lax.ppermute(block, axis, route)


def packed_total(arrays, axis):
    vector, at, gathered = (jnp.concatenate([a.reshape(-1) for a in arrays]), 0, [])
    running = lax.psum(vector, axis)
    for a in arrays:
        gathered.append(running[at : at + a.size].reshape(a.shape))
        at += a.size
    return tuple(gathered)


def cut_along(array, dim, length):
    dims = array.shape
    blocks = array.reshape(*dims[:dim], length, dims[dim] // length, *dims[dim + 1 :])
    return jnp.moveaxis(blocks, dim, 0)


def sent_and_summed(array, axis, dim):
    blocks = cut_along(array, dim, lax.axis_size(axis))
    arrived = lax.all_to_all(blocks, axis, split_axis=0, concat_axis=0, tiled=True)
    return arrived.astype(jnp.float32).sum(axis=0)


def sum_together(arrays, axis, dims):
    length = lax.axis_size(axis)
    blocks = [cut_along(a, dim, length) for a, dim in zip(arrays, dims)]
    lines = jnp.concatenate([b.reshape(length, -1) for b in blocks], axis=1)
    span = max(16, -(-lines.shape[1] // 1024) * 8)
    lines = jnp.pad(lines, ((0, 0), (0, span * 128 - lines.shape[1]))).reshape(-1, 128)
    vector, at, gathered = (lax.psum_scatter(lines, axis, tiled=True).reshape(-1), 0, [])
    for b in blocks:
        part = b[0]
        gathered.append(vector[at : at + part.size].reshape(part.shape))
        at += part.size
    return tuple(gathered)


def lookup(time_table, time_index):
    onehot = (jnp.arange(time_table.shape[0], dtype=jnp.int32) == time_index).astype(jnp.float32)
    return jnp.dot(onehot, time_table, precision=PRECISE)


def project_in(current, norm_gain, condition, weight):
    inv_rms = lax.rsqrt(jnp.mean(current * current, -1, keepdims=True) + EPSILON)
    modulation = norm_gain * (1.0 + condition)
    normed = (current * inv_rms * modulation).astype(jnp.bfloat16)
    qkv_rows = jnp.einsum("nd,dhe->nhe", normed, weight, preferred_element_type=jnp.float32).astype(
        jnp.bfloat16
    )
    return (normed, inv_rms, modulation, qkv_rows)


def attend(queries, key_rows, value_rows, key_mask):
    factor = queries.shape[-1] ** (-0.5)
    scores = (
        jnp.einsum("nhe,lhe->hnl", queries, key_rows, preferred_element_type=jnp.float32) * factor
    )
    scores = jnp.where(key_mask[None], scores, -1e30)
    shifted = jnp.exp(scores - jnp.max(scores, -1, keepdims=True))
    attn_prob = shifted / jnp.sum(shifted, -1, keepdims=True)
    rounded = attn_prob.astype(jnp.bfloat16)
    result = jnp.einsum(
        "hnl,lhe->nhe", rounded, value_rows, preferred_element_type=jnp.float32
    ).astype(jnp.bfloat16)
    return (result, attn_prob, rounded)


def attend_back(queries, key_rows, value_rows, attn_prob, rounded, grad_out):
    factor = queries.shape[-1] ** (-0.5)
    grad_prob = jnp.einsum("nhe,lhe->hnl", grad_out, value_rows, preferred_element_type=jnp.float32)
    center = jnp.sum(attn_prob * grad_prob, -1, keepdims=True)
    dscore = (attn_prob * (grad_prob - center) * factor).astype(jnp.bfloat16)
    dquery = jnp.einsum("hnl,lhe->nhe", dscore, key_rows, preferred_element_type=jnp.float32)
    key_grad = jnp.einsum("hnl,nhe->lhe", dscore, queries, preferred_element_type=jnp.float32)
    value_grad = jnp.einsum("hnl,nhe->lhe", rounded, grad_out, preferred_element_type=jnp.float32)
    return (dquery, key_grad, value_grad)


def norm_back(current, inv_rms, modulation, grad_normed):
    scaled = grad_normed * modulation
    return inv_rms * scaled - current * inv_rms**3 * jnp.mean(scaled * current, -1, keepdims=True)


def local(
    video_tokens,
    audio_tokens,
    qkv_video,
    out_video,
    qkv_audio,
    out_audio,
    gain_video,
    gain_audio,
    time_from,
    time_to,
    time_steps,
    windows,
    intersection,
):
    tokens = video_tokens.shape[1]
    head_dim = out_video.shape[1]
    all_tokens = lax.axis_size("vid") * tokens
    offset = lax.axis_index("vid") * tokens
    query_pos = offset + jnp.arange(tokens, dtype=jnp.int32)
    key_pos = offset - tokens + jnp.arange(3 * tokens, dtype=jnp.int32)
    inside = (key_pos >= 0) & (key_pos < all_tokens)
    distance = jnp.abs(query_pos[:, None] - key_pos[None, :])
    query_blk = query_pos // BLK
    key_blk = jnp.clip(key_pos, 0, all_tokens - 1) // BLK
    low_block = intersection[0, :, 0]
    high_block = intersection[0, :, 1]
    video_cross = (
        inside[None, :]
        & (key_blk[None, :] >= low_block[query_blk][:, None])
        & (key_blk[None, :] < high_block[query_blk][:, None])
    )
    audio_cross = (
        inside[None, :]
        & (query_blk[:, None] >= low_block[key_blk][None, :])
        & (query_blk[:, None] < high_block[key_blk][None, :])
    )
    mask_video = jnp.concatenate([inside[None, :] & (distance < windows[0, 0]), video_cross], 1)
    mask_audio = jnp.concatenate([audio_cross, inside[None, :] & (distance < windows[0, 1])], 1)

    def network(video_now, audio_now, condition):
        video_norm, video_inv, video_mod, video_rows = project_in(
            video_now, gain_video, condition, qkv_video
        )
        audio_norm, audio_inv, audio_mod, audio_rows = project_in(
            audio_now, gain_audio, condition, qkv_audio
        )
        stacked = jnp.stack(
            [
                video_rows[:, :, head_dim:].reshape(tokens, -1),
                audio_rows[:, :, head_dim:].reshape(tokens, -1),
            ]
        )
        widened = padded(stacked, (("vid", 1),), tokens)
        widened = widened.reshape(2, widened.shape[1], -1, 2 * head_dim)
        key_rows = jnp.concatenate([widened[0, :, :, :head_dim], widened[1, :, :, :head_dim]], 0)
        value_rows = jnp.concatenate([widened[0, :, :, head_dim:], widened[1, :, :, head_dim:]], 0)
        video_out, video_prob, video_round = attend(
            video_rows[:, :, :head_dim], key_rows, value_rows, mask_video
        )
        audio_out, audio_prob, audio_round = attend(
            audio_rows[:, :, :head_dim], key_rows, value_rows, mask_audio
        )
        video_part = jnp.einsum(
            "nhe,hef->nf", video_out, out_video, preferred_element_type=jnp.float32
        )
        audio_part = jnp.einsum(
            "nhe,hef->nf", audio_out, out_audio, preferred_element_type=jnp.float32
        )
        video_field, audio_field = (
            lax.psum(video_part.astype(jnp.bfloat16), "aud").astype(jnp.float32),
            lax.psum(audio_part.astype(jnp.bfloat16), "aud").astype(jnp.float32),
        )
        saved = (
            video_norm,
            video_inv,
            video_mod,
            video_rows,
            audio_norm,
            audio_inv,
            audio_mod,
            audio_rows,
            key_rows,
            value_rows,
            video_out,
            video_prob,
            video_round,
            audio_out,
            audio_prob,
            audio_round,
        )
        return (video_field, audio_field, saved)

    start_video = video_tokens[0].astype(jnp.float32)
    start_audio = audio_tokens[0].astype(jnp.float32)
    time_now = time_steps[0, 0]
    stride = time_steps[0, 1]
    euler_step = -stride.astype(jnp.float32) / TGRID
    video_now, audio_now = (start_video, start_audio)
    for teacher_step in range(STEPS):
        time_level = time_now - teacher_step * stride
        condition = lookup(time_from, time_level) + lookup(time_to, time_level)
        video_field, audio_field, unused = network(video_now, audio_now, condition)
        video_now = video_now + euler_step * video_field
        audio_now = audio_now + euler_step * audio_field
    condition = lookup(time_from, time_now) + lookup(time_to, time_now - STEPS * stride)
    video_field, audio_field, saved = network(start_video, start_audio, condition)
    (
        video_norm,
        video_inv,
        video_mod,
        video_rows,
        audio_norm,
        audio_inv,
        audio_mod,
        audio_rows,
        key_rows,
        value_rows,
        video_out,
        video_prob,
        video_round,
        audio_out,
        audio_prob,
        audio_round,
    ) = saved
    span_time = -(STEPS * stride).astype(jnp.float32) / TGRID
    video_diff = start_video + span_time * video_field - video_now
    audio_diff = start_audio + span_time * audio_field - audio_now
    video_grad = (span_time * video_diff).astype(jnp.bfloat16)
    audio_grad = (span_time * audio_diff).astype(jnp.bfloat16)
    video_wout = jnp.einsum(
        "nhe,nf->hef", video_out, video_grad, preferred_element_type=jnp.float32
    )
    audio_wout = jnp.einsum(
        "nhe,nf->hef", audio_out, audio_grad, preferred_element_type=jnp.float32
    )
    video_dout = jnp.einsum(
        "nf,hef->nhe", video_grad, out_video, preferred_element_type=jnp.float32
    ).astype(jnp.bfloat16)
    audio_dout = jnp.einsum(
        "nf,hef->nhe", audio_grad, out_audio, preferred_element_type=jnp.float32
    ).astype(jnp.bfloat16)
    video_dq, video_dk, video_dv = attend_back(
        video_rows[:, :, :head_dim], key_rows, value_rows, video_prob, video_round, video_dout
    )
    audio_dq, audio_dk, audio_dv = attend_back(
        audio_rows[:, :, :head_dim], key_rows, value_rows, audio_prob, audio_round, audio_dout
    )
    length = key_rows.shape[0] // 2
    key_grads = jnp.concatenate([video_dk + audio_dk, video_dv + audio_dv], -1).reshape(
        2, length, -1
    )
    from_right = shifted_2(key_grads[:, :tokens].astype(jnp.bfloat16), "vid", -1).astype(
        jnp.float32
    )
    from_left = shifted_2(key_grads[:, 2 * tokens :].astype(jnp.bfloat16), "vid", 1).astype(
        jnp.float32
    )
    owned = key_grads[:, tokens : 2 * tokens] + from_right + from_left
    owned = owned.reshape(2, tokens, -1, 2 * head_dim)
    video_dqkv = jnp.concatenate([video_dq, owned[0]], -1).astype(jnp.bfloat16)
    audio_dqkv = jnp.concatenate([audio_dq, owned[1]], -1).astype(jnp.bfloat16)
    video_wqkv = jnp.einsum(
        "nd,nhe->dhe", video_norm, video_dqkv, preferred_element_type=jnp.float32
    )
    audio_wqkv = jnp.einsum(
        "nd,nhe->dhe", audio_norm, audio_dqkv, preferred_element_type=jnp.float32
    )
    video_part = jnp.einsum(
        "nhe,dhe->nd", video_dqkv, qkv_video, preferred_element_type=jnp.float32
    )
    audio_part = jnp.einsum(
        "nhe,dhe->nd", audio_dqkv, qkv_audio, preferred_element_type=jnp.float32
    )
    video_back, audio_back = tuple(
        (
            part.astype(jnp.float32)
            for part in packed_total(
                (video_part.astype(jnp.bfloat16), audio_part.astype(jnp.bfloat16)), "aud"
            )
        )
    )
    d_video = (video_diff + norm_back(start_video, video_inv, video_mod, video_back)).astype(
        jnp.bfloat16
    )
    d_audio = (audio_diff + norm_back(start_audio, audio_inv, audio_mod, audio_back)).astype(
        jnp.bfloat16
    )
    first = (
        sent_and_summed(video_wqkv.astype(jnp.bfloat16), "clip", 0),
        sent_and_summed(video_wout.astype(jnp.bfloat16), "clip", 2),
        sent_and_summed(audio_wqkv.astype(jnp.bfloat16), "clip", 0),
        sent_and_summed(audio_wout.astype(jnp.bfloat16), "clip", 2),
    )
    summed = tuple(
        (
            part.astype(jnp.float32)
            for part in sum_together(
                (
                    first[0].astype(jnp.bfloat16),
                    first[1].astype(jnp.bfloat16),
                    first[2].astype(jnp.bfloat16),
                    first[3].astype(jnp.bfloat16),
                ),
                "vid",
                (0, 2, 0, 2),
            )
        )
    )
    return (d_video[None], d_audio[None], summed[0], summed[1], summed[2], summed[3])


def solution(mesh):
    return jax.shard_map(
        local,
        mesh=mesh,
        in_specs=(
            P("clip", "vid", None),
            P("clip", "vid", None),
            P(None, "aud", None),
            P("aud", None, None),
            P(None, "aud", None),
            P("aud", None, None),
            P(),
            P(),
            P(),
            P(),
            P("clip", None),
            P("clip", None),
            P("clip", None, None),
        ),
        out_specs=(
            P("clip", "vid", None),
            P("clip", "vid", None),
            P(("clip", "vid"), "aud", None),
            P("aud", None, ("clip", "vid")),
            P(("clip", "vid"), "aud", None),
            P("aud", None, ("clip", "vid")),
        ),
        check_vma=False,
    )
```

profile of v0, /device:TPU:1, one launch (start us, length us, event | category | flops | bytes accessed | tf_op | source)
XLA Modules:
  0.0 881.5 jit_solution(6842922435043342061)
XLA Ops:
  29.4 5.1 collective-permute-start.1
  48.0 3.1 collective-permute-start.3
  77.4 4.4 fusion.221
  81.8 4.4 fusion.220
  86.2 16.3 %select_select_fusion.1 = s32[384]{0:T(512)S(1)} fusion(pred[384]{0:T(512)(128)(4,1)} %compare_reduce_fusion, pred[384]{0:T(512)(128)(4,1)} %compare_reduce_fusion.1, pred[384]{0:T(512)(128)(4,1)} %compare_reduce_fusion.2, pred[384]{0:T(512)(128)(4,1)} %compare_reduce_fusion.3, pred[384]{0:T(512)(128)(4,1)} %compare_reduce_fusion.4, ...), kind=kLoop, calls=%fused_computation.310 | loop fusion | flops 9600 | bytes 12772 | tf_op jit(solution)/shard_map/gather | solution.py:149
  102.5 16.4 %select_select_fusion = s32[384]{0:T(512)S(1)} fusion(pred[384]{0:T(512)(128)(4,1)} %compare_reduce_fusion, pred[384]{0:T(512)(128)(4,1)} %compare_reduce_fusion.1, pred[384]{0:T(512)(128)(4,1)} %compare_reduce_fusion.2, pred[384]{0:T(512)(128)(4,1)} %compare_reduce_fusion.3, pred[384]{0:T(512)(128)(4,1)} %compare_reduce_fusion.4, ...), kind=kLoop, calls=%fused_computation.309 | loop fusion | flops 9600 | bytes 12772 | tf_op jit(solution)/shard_map/gather | solution.py:150
  144.0 3.5 fusion.9
  147.5 3.5 fusion.10
  164.0 120.6 %all-reduce.10.cloned.1.call-done = (bf16[128,2048]{1,0:T(8,128)(2,1)}, bf16[128,2048]{1,0:T(8,128)(2,1)}) async-done(((bf16[128,2048]{1,0:T(8,128)(2,1)}, bf16[128,2048]{1,0:T(8,128)(2,1)}), (bf16[128,2048]{1,0:T(8,128)(2,1)}, bf16[128,2048]{1,0:T(8,128)(2,1)})) %all-reduce.10.cloned.1.call-update) | async-done | bytes 1048592 | tf_op jit(solution)/shard_map/psum | solution.py:186
  300.1 5.2 collective-permute-start.5
  324.3 3.5 fusion.11
  327.8 3.5 fusion.13
  331.4 193.0 %all-reduce.8.cloned.1.call-done = (bf16[128,2048]{1,0:T(8,128)(2,1)}, bf16[128,2048]{1,0:T(8,128)(2,1)}, bf16[128,2048]{1,0:T(8,128)(2,1)}, bf16[128,2048]{1,0:T(8,128)(2,1)}) async-done(((bf16[128,2048]{1,0:T(8,128)(2,1)}, bf16[128,2048]{1,0:T(8,128)(2,1)}, bf16[128,2048]{1,0:T(8,128)(2,1)}, bf16[128,2048]{1,0:T(8,128)(2,1)}), (bf16[128,2048]{1,0:T(8,128)(2,1)}, bf16[128,2048]{1,0:T(8,128)(2,1)}, ...) | async-done | bytes 2097168 | tf_op jit(solution)/shard_map/psum | solution.py:185
  524.3 3.9 fusion.125
  530.9 4.5 all-to-all-start.3
  544.4 4.0 fusion.116
  548.4 4.2 fusion.49
  552.6 8.1 all-to-all-done.3
  560.7 4.3 all-to-all-start.1
  565.0 3.0 fusion.48
  576.1 3.3 collective-permute-start.6
  583.6 3.6 fusion.90
  593.5 4.7 all-to-all-start
  598.3 3.6 fusion.93
  611.1 57.8 %all-to-all-done = bf16[4,512,2,384]{3,1,2,0:T(8,128)(2,1)} async-done(((bf16[4,512,2,384]{3,1,2,0:T(8,128)(2,1)}), bf16[4,512,2,384]{3,1,2,0:T(8,128)(2,1)}, u32[]{:S(2)}, u32[]{:S(2)}) %all-to-all-start) | async-done | bytes 3145760 | tf_op jit(solution)/shard_map/all_to_all | solution.py:51
  668.9 4.6 all-to-all-start.2
  690.1 3.5 reduce_sum.196
  699.0 87.1 %all-to-all-done.2 = bf16[4,512,2,384]{3,1,2,0:T(8,128)(2,1)} async-done(((bf16[4,512,2,384]{3,1,2,0:T(8,128)(2,1)}), bf16[4,512,2,384]{3,1,2,0:T(8,128)(2,1)}, u32[]{:S(2)}, u32[]{:S(2)}) %all-to-all-start.2) | async-done | bytes 3145760 | tf_op jit(solution)/shard_map/all_to_all | solution.py:51
  786.1 3.5 reduce_sum.198
  797.9 3.9 reshape.357
  801.8 22.6 %all-reduce.6.cloned.1.call-done = bf16[524288]{0:T(1024)(128)(2,1)} async-done(((bf16[524288]{0:T(1024)(128)(2,1)}), bf16[524288]{0:T(1024)(128)(2,1)}) %all-reduce.6.cloned.1.call-update) | async-done | bytes 1048592 | tf_op jit(solution)/shard_map/psum | solution.py:36
  839.9 29.7 %reduce-scatter.2.cloned.1.call-done = bf16[1024,128]{1,0:T(8,128)(2,1)} async-done(((bf16[8192,128]{1,0:T(8,128)(2,1)}), bf16[1024,128]{1,0:T(8,128)(2,1)}) %reduce-scatter.2.cloned.1.call-update) | async-done | bytes 262160 | tf_op jit(solution)/shard_map/reduce_scatter | solution.py:61
  (285 shorter events, 221.0 us)
Async XLA Ops:
  7.2 15.3 %copy-start = (bf16[2048,2,384]{2,1,0:T(2,128)(2,1)S(1)}, bf16[2048,2,384]{2,1,0:T(2,128)(2,1)}, u32[]{:S(2)}) copy-start(bf16[2048,2,384]{2,1,0:T(2,128)(2,1)} %param.17) | copy-start | bytes 9437188
  7.2 14.7 %copy-start.34 = (f32[2048]{0:T(1024)S(1)}, f32[2048]{0:T(1024)}, u32[]{:S(2)}) copy-start(f32[2048]{0:T(1024)} %param.20) | copy-start | bytes 24580
  7.2 14.7 %copy-start.33 = (f32[2048]{0:T(1024)S(1)}, f32[2048]{0:T(1024)}, u32[]{:S(2)}) copy-start(f32[2048]{0:T(1024)} %param.19) | copy-start | bytes 24580
  7.2 277.4 %all-reduce.10.cloned.1.call-start = ((), (), s32[]{:S(2)}) async-start(), calls=%async_computation.8 | async-start | bytes 2097152 | tf_op jit(solution)/shard_map/psum | solution.py:186
  9.9 8.1 copy-start.1
  28.7 12.9 %copy-start.37 = (f32[2048]{0:T(1024)S(1)}, f32[2048]{0:T(1024)}, u32[]{:S(2)}) copy-start(f32[2048]{0:T(1024)} %get-tuple-element.59) | copy-start | bytes 24580
  29.4 109.1 %collective-permute-start.1 = (bf16[2,128,512]{1,2,0:T(8,128)(2,1)}, bf16[2,128,512]{1,2,0:T(8,128)(2,1)}, u32[]{:S(2)}, u32[]{:S(2)}) collective-permute-start(bf16[2,128,512]{1,2,0:T(8,128)(2,1)} %pad_maximum_fusion.12), channel_id=1, source_target_pairs={{8,0},{16,8},{24,16},{32,24},{40,32},{48,40},{56,48},{9,1},{17,9},... | collective-permute-start | bytes 786440 | tf_op jit(solution)/shard_map/ppermute | solution.py:23
  34.5 104.0 %collective-permute-start = (bf16[2,128,512]{1,2,0:T(8,128)(2,1)}, bf16[2,128,512]{1,2,0:T(8,128)(2,1)}, u32[]{:S(2)}, u32[]{:S(2)}) collective-permute-start(bf16[2,128,512]{1,2,0:T(8,128)(2,1)} %pad_maximum_fusion.12), channel_id=1, source_target_pairs={{0,8},{8,16},{16,24},{24,32},{32,40},{40,48},{48,56},{1,9},{9,17},... | collective-permute-start | bytes 786440 | tf_op jit(solution)/shard_map/ppermute | solution.py:20
  41.6 28.6 %copy-start.14 = (s32[1,32,2]{1,2,0:T(2,128)S(1)}, s32[1,32,2]{1,2,0:T(2,128)}, u32[]{:S(2)}) copy-start(s32[1,32,2]{1,2,0:T(2,128)} %param.25) | copy-start | bytes 772
  48.0 77.3 %collective-permute-start.3 = (bf16[2,128,512]{1,2,0:T(8,128)(2,1)}, bf16[2,128,512]{1,2,0:T(8,128)(2,1)}, u32[]{:S(2)}, u32[]{:S(2)}) collective-permute-start(bf16[2,128,512]{1,2,0:T(8,128)(2,1)} %pad_maximum_fusion.13), channel_id=1, source_target_pairs={{8,0},{16,8},{24,16},{32,24},{40,32},{48,40},{56,48},{9,1},{17,9},... | collective-permute-start | bytes 786440 | tf_op jit(solution)/shard_map/ppermute | solution.py:23
  51.1 74.2 %collective-permute-start.2 = (bf16[2,128,512]{1,2,0:T(8,128)(2,1)}, bf16[2,128,512]{1,2,0:T(8,128)(2,1)}, u32[]{:S(2)}, u32[]{:S(2)}) collective-permute-start(bf16[2,128,512]{1,2,0:T(8,128)(2,1)} %pad_maximum_fusion.13), channel_id=1, source_target_pairs={{0,8},{8,16},{16,24},{24,32},{32,40},{40,48},{48,56},{1,9},{9,17},... | collective-permute-start | bytes 786440 | tf_op jit(solution)/shard_map/ppermute | solution.py:20
  126.5 8.3 copy-start.26
  151.1 373.3 %all-reduce.8.cloned.1.call-start = ((), (), s32[]{:S(2)}) async-start(), calls=%async_computation.7 | async-start | bytes 4194304 | tf_op jit(solution)/shard_map/psum | solution.py:185
  159.2 128.9 %copy-start.36 = (f32[2048]{0:T(1024)S(1)}, f32[2048]{0:T(1024)}, u32[]{:S(2)}) copy-start(f32[2048]{0:T(1024)} %get-tuple-element.56) | copy-start | bytes 24580
  300.1 10.0 %collective-permute-start.5 = (bf16[2,128,512]{1,2,0:T(8,128)(2,1)S(1)}, bf16[2,128,512]{1,2,0:T(8,128)(2,1)S(1)}, u32[]{:S(2)}, u32[]{:S(2)}) collective-permute-start(bf16[2,128,512]{1,2,0:T(8,128)(2,1)S(1)} %pad_maximum_fusion.14), channel_id=1, source_target_pairs={{8,0},{16,8},{24,16},{32,24},{40,32},{48,40},{56,48},{9,1},{17,9},... | collective-permute-start | bytes 786440 | tf_op jit(solution)/shard_map/ppermute | solution.py:23
  305.4 5.7 collective-permute-start.4
  530.9 29.8 %all-to-all-start.3 = ((bf16[4,2,128,512]{3,2,1,0:T(8,128)(2,1)}), bf16[4,2,128,512]{3,2,1,0:T(8,128)(2,1)}, u32[]{:S(2)}, u32[]{:S(2)}) async-start(bf16[4,2,128,512]{3,2,1,0:T(8,128)(2,1)} %bitcast.327), calls=%async_computation.3 | async-start | bytes 2097152 | tf_op jit(solution)/shard_map/all_to_all | solution.py:51
  541.5 6.8 copy-start.46
  548.4 16.6 %copy-start.19 = (bf16[128,2,128]{2,0,1:T(8,128)(2,1)S(1)}, bf16[128,2,128]{2,0,1:T(8,128)(2,1)}, u32[]{:S(2)}) copy-start(bf16[128,2,128]{2,0,1:T(8,128)(2,1)} %convolution_convert_fusion.5) | copy-start | bytes 196612
  548.4 16.6 %copy-start.21 = (bf16[1,384,2,128]{3,1,2,0:T(8,128)(2,1)S(1)}, bf16[1,384,2,128]{3,1,2,0:T(8,128)(2,1)}, u32[]{:S(2)}) copy-start(bf16[1,384,2,128]{3,1,2,0:T(8,128)(2,1)} %copy.219) | copy-start | bytes 589828
  560.7 32.8 %all-to-all-start.1 = ((bf16[4,2,128,512]{3,2,1,0:T(8,128)(2,1)}), bf16[4,2,128,512]{3,2,1,0:T(8,128)(2,1)}, u32[]{:S(2)}, u32[]{:S(2)}) async-start(bf16[4,2,128,512]{3,2,1,0:T(8,128)(2,1)} %bitcast.326), calls=%async_computation.1 | async-start | bytes 2097152 | tf_op jit(solution)/shard_map/all_to_all | solution.py:51
  573.6 8.8 copy-start.5
  573.6 10.0 %copy-start.49 = (f32[2,128]{1,0:T(2,128)S(1)}, f32[2,128]{1,0:T(2,128)}, u32[]{:S(2)}) copy-start(f32[2,128]{1,0:T(2,128)} %copy-done.47) | copy-start | bytes 3076
  576.1 11.9 %collective-permute-start.6 = (bf16[2,128,512]{1,2,0:T(8,128)(2,1)}, bf16[2,128,512]{1,2,0:T(8,128)(2,1)S(1)}, u32[]{:S(2)}, u32[]{:S(2)}) collective-permute-start(bf16[2,128,512]{1,2,0:T(8,128)(2,1)} %get-tuple-element.32), channel_id=1, source_target_pairs={{8,0},{16,8},{24,16},{32,24},{40,32},{48,40},{56,48},{9,1},{17,9},... | collective-permute-start | bytes 786440 | tf_op jit(solution)/shard_map/ppermute | solution.py:31
  579.4 8.6 collective-permute-start.7
  593.5 75.3 %all-to-all-start = ((bf16[4,512,2,384]{3,1,2,0:T(8,128)(2,1)}), bf16[4,512,2,384]{3,1,2,0:T(8,128)(2,1)}, u32[]{:S(2)}, u32[]{:S(2)}) async-start(bf16[4,512,2,384]{3,1,2,0:T(8,128)(2,1)} %copy.180), calls=%async_computation | async-start | bytes 6291456 | tf_op jit(solution)/shard_map/all_to_all | solution.py:51
  668.9 117.2 %all-to-all-start.2 = ((bf16[4,512,2,384]{3,1,2,0:T(8,128)(2,1)}), bf16[4,512,2,384]{3,1,2,0:T(8,128)(2,1)}, u32[]{:S(2)}, u32[]{:S(2)}) async-start(bf16[4,512,2,384]{3,1,2,0:T(8,128)(2,1)} %copy.188), calls=%async_computation.2 | async-start | bytes 6291456 | tf_op jit(solution)/shard_map/all_to_all | solution.py:51
  673.5 150.9 %all-reduce.6.cloned.1.call-start = ((), (), s32[]{:S(2)}) async-start(), calls=%async_computation.5 | async-start | bytes 2097152 | tf_op jit(solution)/shard_map/psum | solution.py:36
  675.9 193.6 %reduce-scatter.2.cloned.1.call-start = ((), (), s32[]{:S(2)}) async-start(), calls=%async_computation.6 | async-start | bytes 2359296 | tf_op jit(solution)/shard_map/reduce_scatter | solution.py:61
  831.8 6.5 copy-start.4
  831.8 6.5 copy-start.6
  831.8 6.5 copy-start.8
  (34 other events, 121.4 us)
Sparse Core Ops, SparseCore 0:
  151.2 133.3 all-reduce.9
  331.5 192.8 all-reduce.7
  677.0 147.3 all-reduce.5
  826.8 42.7 reduce-scatter.1
where the time goes:
time: 894 us; the launch traced here: 881 us
  waiting for transfers between devices  520 us (58%)
  other arithmetic  113 us (13%)
  matrix products  100 us (11%)
  local copies, waits for them, and re-layouts  85.4 us (10%)
  starting transfers between devices  45.1 us (5%)
  between operations  18 us (2%)
    psum x1, waiting for transfers between devices, network(): lax.psum(video_part.astype(jnp.bfloat16), 'aud').astype(jnp.float32)  193 us
    all_to_all x4, waiting for transfers between devices, sent_and_summed(): lax.all_to_all(blocks, axis, split_axis=0, concat_axis=0, tiled=True)  153 us
    psum x1, waiting for transfers between devices, network(): lax.psum(audio_part.astype(jnp.bfloat16), 'aud').astype(jnp.float32)  121 us
    gather x27, other arithmetic, local(): low_block[key_blk][None, :]  35 us
    reduce_scatter x1, waiting for transfers between devices, sum_together(): lax.psum_scatter(lines, axis, tiled=True).reshape(-1)  29.7 us
    psum x1, waiting for transfers between devices, packed_total(): running = lax.psum(vector, axis)  22.6 us
    gather x2, other arithmetic, local(): high_block[key_blk][None, :]  20.8 us
    unnamed x110, local copies, waits for them, and re-layouts  19.1 us
  transfers between devices with their start and end apart: 16, of which 8 were waited for; matrix products, arithmetic and copies ran while one was open for 25% of the time, Pallas kernels for 0%

commit v1 on v0

v1 whole, which is shorter than its diff:
```python
import jax
import jax.numpy as jnp
from jax import lax
from jax.experimental import pallas as pl
from jax.experimental.pallas import tpu as pltpu
from jax.sharding import PartitionSpec as P

BLK = 32
TGRID = 64
STEPS = 2
EPSILON = 1e-06
MESH = pl.DeviceIdType.MESH
F32 = jnp.float32
BF16 = jnp.bfloat16
NT = (((1,), (1,)), ((), ()))
TN = (((0,), (0,)), ((), ()))
NN = (((1,), (0,)), ((), ()))
T1, ST, T2 = 0, 1, 2


def dot(a, b, dims):
    return lax.dot_general(a, b, dims, preferred_element_type=F32)


def kernel(
    xv, xa, mods, bias, wqv, wqa, wov, woa,
    dv_out, da_out, g_out,
    WQ, WO, N0, NS, NG, OB, OG, GS, GG, DQ, DG, QR, KV, PS, ACC, SB, R1, S2, R2, ZS, ZR, AG, DIFF,
    DO, DKV, DKS, DKR, W1, WR1, W2, WR2, SW, RW,
    w_sem, o_sem, kv_s, kv_r, ar_s, ar_r, ng_s, ng_r, og_s, og_r, gg_s, gg_r, dg_s, dg_r,
    w1_s, w1_r, w2_s, w2_r, sw_s, sw_r,
):
    v = lax.axis_index("vid")
    a = lax.axis_index("aud")
    c = lax.axis_index("clip")
    core = lax.rem(v, 2)
    yy = v // 2
    x = a // 2
    zh = lax.rem(a, 2)
    b0 = lax.rem(x, 2)
    b1 = x // 2
    q = lax.rem(b0 + b1, 2)
    near = (x + 1 - 2 * b0) * 2 + zh
    far = (3 - x) * 2 + zh
    across = a + 1 - 2 * zh
    first = (near, far)
    second = (far, near)
    keep1 = (q, b1)
    keep2 = (b1, b0)
    right = lax.rem(v + 1, 8)
    left = lax.rem(v + 7, 8)
    half0 = [pl.multiple_of(64 * k, 64) for k in keep1]
    half1 = [pl.multiple_of(64 * (1 - k), 64) for k in keep1]
    own = [pl.multiple_of(64 * k + 32 * j, 32) for k, j in zip(keep1, keep2)]
    other = [pl.multiple_of(64 * k + 32 * (1 - j), 32) for k, j in zip(keep1, keep2)]
    own_in = [pl.multiple_of(32 * j, 32) for j in keep2]
    other_in = [pl.multiple_of(32 * (1 - j), 32) for j in keep2]

    loads = [
        pltpu.make_async_copy(wqv, WQ.at[0], w_sem.at[0]),
        pltpu.make_async_copy(wqa, WQ.at[1], w_sem.at[1]),
        pltpu.make_async_copy(wov, WO.at[0], w_sem.at[2]),
        pltpu.make_async_copy(woa, WO.at[1], w_sem.at[3]),
    ]
    for load in loads:
        load.start()

    barrier = pltpu.get_barrier_semaphore()
    for d in range(1, 8):
        pl.semaphore_signal(barrier, 1, device_id={"vid": lax.rem(v + d, 8)}, device_id_type=MESH)
    for peer in (near, far, across):
        pl.semaphore_signal(barrier, 1, device_id={"aud": peer}, device_id_type=MESH)
    for d in range(1, 4):
        pl.semaphore_signal(barrier, 1, device_id={"clip": lax.rem(c + d, 4)}, device_id_type=MESH)

    pending = []

    def remote(src, dst, send, recv, device):
        return pltpu.make_async_remote_copy(
            src_ref=src, dst_ref=dst, send_sem=send, recv_sem=recv, device_id=device, device_id_type=MESH
        )

    def go(copy):
        copy.start()
        pending.append(copy)

    xs = (xv, xa)
    for m in range(2):

        def norm_rows(r, carry, m=m):
            rows = pl.ds(pl.multiple_of(r * 32, 32), 32)
            cur = xs[m][rows, :].astype(F32)
            inv = lax.rsqrt(jnp.mean(cur * cur, -1, keepdims=True) + EPSILON)
            scaled = cur * inv
            N0[m, 0, rows, :] = (scaled * mods[m : m + 1, :]).astype(BF16)
            student = (scaled * mods[2 + m : 3 + m, :]).astype(BF16)
            N0[m, 1, rows, :] = student
            for s in range(16):
                NS[m, s // 4, s % 4, rows, :] = student[:, 128 * s : 128 * s + 128]
            return carry

        lax.fori_loop(0, 4, norm_rows, 0)

    def store_qkv(net, m, rows):
        rounded = rows.astype(BF16)
        for h in range(2):
            QR[net, m, :, 128 * h : 128 * h + 128] = rounded[:, 384 * h : 384 * h + 128]
            KV[net, 1, m, :, 256 * h : 256 * h + 256] = rounded[:, 384 * h + 128 : 384 * h + 384]

    for m in range(2):
        loads[m].wait()
        both = dot(N0[m].reshape(256, 2048), WQ[m], NN)
        store_qkv(T1, m, both[:128])
        store_qkv(ST, m, both[128:])

    pl.semaphore_wait(barrier, 13)

    def kv_copies(net):
        return (
            remote(KV.at[net, 1], KV.at[net, 0], kv_s.at[2 * net], kv_r.at[2 * net], {"vid": right}),
            remote(KV.at[net, 1], KV.at[net, 2], kv_s.at[2 * net + 1], kv_r.at[2 * net + 1], {"vid": left}),
        )

    def kv_start(net):
        for copy in kv_copies(net):
            go(copy)

    def kv_wait(net):
        for copy in kv_copies(net):
            copy.wait_recv()

    kv_start(T1)
    kv_start(ST)

    def spread(src, dst, send, recv):
        for d in range(1, 8):
            peer = lax.rem(v + d, 8)
            go(remote(src(lax.rem(peer, 2), peer // 2), dst.at[v], send.at[peer], recv.at[v], {"vid": peer}))

    def collect(dst, send, recv):
        for d in range(1, 8):
            peer = lax.rem(v + d, 8)
            remote(dst.at[peer], dst.at[peer], send.at[peer], recv.at[peer], {"vid": peer}).wait_recv()

    NG[v] = NS[core, :, yy]
    spread(lambda k, y: NS.at[k, :, y], NG, ng_s, ng_r)

    factor = 128 ** (-0.5)

    def attention(net, m, save):
        for h in range(2):
            queries = QR[net, m, :, 128 * h : 128 * h + 128]
            keys = KV[net, :, :, :, 256 * h : 256 * h + 128].reshape(768, 128)
            values = KV[net, :, :, :, 256 * h + 128 : 256 * h + 256].reshape(768, 128)
            scores = dot(queries, keys, NT) * factor + bias[m]
            shifted = jnp.exp(scores - jnp.max(scores, -1, keepdims=True))
            prob = shifted * (1.0 / jnp.sum(shifted, -1, keepdims=True))
            if save:
                PS[2 * m + h] = prob
            OB[net, m, :, 128 * h : 128 * h + 128] = dot(prob.astype(BF16), values, NN).astype(BF16)

    def project_out(net, m):
        return dot(OB[net, m], WO[m], NN)

    def ar1(i, m):
        return remote(
            SB.at[i, m, pl.ds(half1[m], 64)], R1.at[i, m], ar_s.at[i, m, 0], ar_r.at[i, m, 0], {"aud": first[m]}
        )

    def ar2(i, m):
        return remote(S2.at[i, m], R2.at[i, m], ar_s.at[i, m, 1], ar_r.at[i, m, 1], {"aud": second[m]})

    def ar3(i, m):
        return remote(ZS.at[i, m], ZR.at[i, m], ar_s.at[i, m, 2], ar_r.at[i, m, 2], {"aud": across})

    def ag1(i, m):
        part = AG.at[i, m, pl.ds(own[m], 32)]
        return remote(part, part, ar_s.at[i, m, 3], ar_r.at[i, m, 3], {"aud": second[m]})

    def ag2(i, m):
        part = AG.at[i, m, pl.ds(half0[m], 64)]
        return remote(part, part, ar_s.at[i, m, 4], ar_r.at[i, m, 4], {"aud": first[m]})

    def ag1_recv(i, m):
        part = AG.at[i, m, pl.ds(other[m], 32)]
        remote(part, part, ar_s.at[i, m, 3], ar_r.at[i, m, 3], {"aud": second[m]}).wait_recv()

    def ag2_recv(i, m):
        part = AG.at[i, m, pl.ds(half1[m], 64)]
        remote(part, part, ar_s.at[i, m, 4], ar_r.at[i, m, 4], {"aud": first[m]}).wait_recv()

    def wide(ref):
        return ref.astype(F32)

    def reduce_1(i):
        for m in range(2):
            ar1(i, m).wait_recv()
            S2[i, m] = (
                wide(SB[i, m, pl.ds(other[m], 32), :]) + wide(R1[i, m, pl.ds(other_in[m], 32), :])
            ).astype(BF16)
            go(ar2(i, m))

    def reduce_2(i):
        for m in range(2):
            ar2(i, m).wait_recv()
            ZS[i, m] = (
                wide(SB[i, m, pl.ds(own[m], 32), :])
                + wide(R1[i, m, pl.ds(own_in[m], 32), :])
                + wide(R2[i, m])
            ).astype(BF16)
            go(ar3(i, m))

    def reduced(i, m):
        ar3(i, m).wait_recv()
        return wide(ZS[i, m]) + wide(ZR[i, m])

    def share_1(i):
        for m in range(2):
            ag1_recv(i, m)
            go(ag2(i, m))

    def share_2(i):
        for m in range(2):
            ag2_recv(i, m)

    for m in range(2):
        loads[2 + m].wait()
    kv_wait(T1)
    for m in range(2):
        attention(T1, m, False)
        field = project_out(T1, m)
        SB[0, m] = field.astype(BF16)
        ACC[m] = -field
        go(ar1(0, m))
    kv_wait(ST)
    attention(ST, 0, True)
    reduce_1(0)
    attention(ST, 1, True)
    OG[v] = OB[ST, core]
    spread(lambda k, y: OB.at[ST, k], OG, og_s, og_r)
    reduce_2(0)
    for m in range(2):
        ACC[m] = ACC[m] + 2.0 * project_out(ST, m)
    step = mods[6:7, :]
    for m in range(2):
        total = reduced(0, m)
        cur = wide(xs[m][pl.ds(own[m], 32), :]) + step * total
        inv = lax.rsqrt(jnp.mean(cur * cur, -1, keepdims=True) + EPSILON)
        AG[0, m, pl.ds(own[m], 32), :] = (cur * inv * mods[4 + m : 5 + m, :]).astype(BF16)
        go(ag1(0, m))
    share_1(0)
    share_2(0)

    for m in range(2):
        store_qkv(T2, m, dot(AG[0, m], WQ[m], NN))
    kv_start(T2)
    kv_wait(T2)
    for m in range(2):
        attention(T2, m, False)
        SB[1, m] = (ACC[m] - project_out(T2, m)).astype(BF16)
        go(ar1(1, m))
    collect(NG, ng_s, ng_r)
    collect(OG, og_s, og_r)
    reduce_1(1)
    reduce_2(1)
    for m in range(2):
        diff = step * reduced(1, m)
        DIFF[m] = diff
        AG[1, m, pl.ds(own[m], 32), :] = (2.0 * step * diff).astype(BF16)
        go(ag1(1, m))
    share_1(1)
    share_2(1)

    for m in range(2):
        for s in range(16):
            GS[m, s // 4, s % 4] = AG[1, m, :, 128 * s : 128 * s + 128]
    GG[v] = GS[core, :, yy]
    spread(lambda k, y: GS.at[k, :, y], GG, gg_s, gg_r)
    for m in range(2):
        DO[m] = dot(AG[1, m], WO[m], NT).astype(BF16)
    for m in range(2):
        for h in range(2):
            cols = slice(256 * h, 256 * h + 128)
            vcols = slice(256 * h + 128, 256 * h + 256)
            queries = QR[ST, m, :, 128 * h : 128 * h + 128]
            keys = KV[ST, :, :, :, cols].reshape(768, 128)
            values = KV[ST, :, :, :, vcols].reshape(768, 128)
            grad_out = DO[m, :, 128 * h : 128 * h + 128]
            prob = PS[2 * m + h]
            grad_prob = dot(grad_out, values, NT)
            center = jnp.sum(prob * grad_prob, -1, keepdims=True)
            dscore = (prob * (grad_prob - center) * factor).astype(BF16)
            DQ[m, :, 384 * h : 384 * h + 128] = dot(dscore, keys, NN).astype(BF16)
            dkey = dot(dscore, queries, TN).reshape(3, 2, 128, 128)
            dvalue = dot(prob.astype(BF16), grad_out, TN).reshape(3, 2, 128, 128)
            if m == 0:
                DKV[:, :, :, cols] = dkey
                DKV[:, :, :, vcols] = dvalue
            else:
                DKV[:, :, :, cols] = DKV[:, :, :, cols] + dkey
                DKV[:, :, :, vcols] = DKV[:, :, :, vcols] + dvalue
    DKS[0] = DKV[0].astype(BF16)
    DKS[1] = DKV[2].astype(BF16)
    edges = (
        remote(DKS.at[0], DKR.at[0], kv_s.at[6], kv_r.at[6], {"vid": left}),
        remote(DKS.at[1], DKR.at[1], kv_s.at[7], kv_r.at[7], {"vid": right}),
    )
    for copy in edges:
        go(copy)
    for copy in edges:
        copy.wait_recv()
    for m in range(2):
        owned = (DKV[1, m] + wide(DKR[0, m]) + wide(DKR[1, m])).astype(BF16)
        for h in range(2):
            DQ[m, :, 384 * h + 128 : 384 * h + 384] = owned[:, 256 * h : 256 * h + 256]
    DG[v] = DQ[core]
    spread(lambda k, y: DQ.at[k], DG, dg_s, dg_r)
    for m in range(2):
        SB[2, m] = dot(DQ[m], WQ[m], NT).astype(BF16)
        go(ar1(2, m))

    def clip_copies(send, got, s_sem, r_sem):
        for d in range(1, 4):
            peer = lax.rem(c + d, 4)
            go(remote(send.at[peer], got.at[c], s_sem.at[peer], r_sem.at[c], {"clip": peer}))

    def clip_sum(send, got, s_sem, r_sem):
        total = wide(send[c])
        for d in range(1, 4):
            peer = lax.rem(c + d, 4)
            remote(got.at[peer], got.at[peer], s_sem.at[peer], r_sem.at[peer], {"clip": peer}).wait_recv()
            total = total + wide(got[peer])
        return total

    collect(GG, gg_s, gg_r)
    o_all = OG[...].reshape(1024, 256)
    for s in range(4):
        W2[s] = dot(GG[:, s].reshape(1024, 128), o_all, TN).astype(BF16)
    clip_copies(W2, WR2, w2_s, w2_r)
    reduce_1(2)
    reduce_2(2)
    collect(DG, dg_s, dg_r)
    d_all = DG[...].reshape(1024, 768)
    for s in range(4):
        W1[s] = dot(NG[:, s].reshape(1024, 128), d_all, TN).astype(BF16)
    clip_copies(W1, WR1, w1_s, w1_r)
    for m in range(2):
        cur = wide(xs[m][pl.ds(own[m], 32), :])
        inv = lax.rsqrt(jnp.mean(cur * cur, -1, keepdims=True) + EPSILON)
        scaled = reduced(2, m) * mods[2 + m : 3 + m, :]
        back = inv * scaled - cur * (inv * inv * inv) * jnp.mean(scaled * cur, -1, keepdims=True)
        AG[2, m, pl.ds(own[m], 32), :] = (DIFF[m] + back).astype(BF16)
        go(ag1(2, m))
    share_1(2)
    mine = pl.ds(pl.multiple_of(64 * core, 64), 64)
    theirs = pl.ds(pl.multiple_of(64 * (1 - core), 64), 64)
    WS = ACC.at[0]
    WS[:, 768:1024] = clip_sum(W2, WR2, w2_s, w2_r)
    WS[:, 0:768] = clip_sum(W1, WR1, w1_s, w1_r)
    SW[...] = WS[theirs, 0:1024]
    swap = remote(SW, RW, sw_s, sw_r, {"vid": v + 1 - 2 * core})
    go(swap)
    g_out[core] = WS[mine, 0:1024]
    share_2(2)
    outs = (
        pltpu.make_async_copy(AG.at[2, 0], dv_out, o_sem.at[0]),
        pltpu.make_async_copy(AG.at[2, 1], da_out, o_sem.at[1]),
    )
    for copy in outs:
        copy.start()
    swap.wait_recv()
    g_out[1 - core] = RW[...]
    for copy in outs:
        copy.wait()
    for copy in pending:
        copy.wait_send()


def vm(shape, kind=BF16):
    return pltpu.VMEM(shape, kind)


def fused(xv, xa, mods, bias, wqv, wqa, wov, woa):
    dma = pltpu.SemaphoreType.DMA
    inside = pl.BlockSpec(memory_space=pltpu.VMEM)
    outside = pl.BlockSpec(memory_space=pl.ANY)
    return pl.pallas_call(
        kernel,
        out_shape=(
            jax.ShapeDtypeStruct((128, 2048), BF16),
            jax.ShapeDtypeStruct((128, 2048), BF16),
            jax.ShapeDtypeStruct((2, 64, 1024), F32),
        ),
        in_specs=[inside] * 4 + [outside] * 4,
        out_specs=(outside, outside, inside),
        scratch_shapes=[
            vm((2, 2048, 768)), vm((2, 256, 2048)), vm((2, 2, 128, 2048)), vm((2, 4, 4, 128, 128)),
            vm((8, 4, 128, 128)), vm((3, 2, 128, 256)), vm((8, 128, 256)), vm((2, 4, 4, 128, 128)),
            vm((8, 4, 128, 128)), vm((2, 128, 768)), vm((8, 128, 768)), vm((3, 2, 128, 256)),
            vm((3, 3, 2, 128, 512)), vm((4, 128, 768), F32), vm((2, 128, 2048), F32),
            vm((3, 2, 128, 2048)), vm((3, 2, 64, 2048)), vm((3, 2, 32, 2048)), vm((3, 2, 32, 2048)),
            vm((3, 2, 32, 2048)), vm((3, 2, 32, 2048)), vm((3, 2, 128, 2048)), vm((2, 32, 2048), F32),
            vm((2, 128, 256)), vm((3, 2, 128, 512), F32), vm((2, 2, 128, 512)), vm((2, 2, 128, 512)),
            vm((4, 128, 768)), vm((4, 128, 768)), vm((4, 128, 256)), vm((4, 128, 256)),
            vm((64, 1024), F32), vm((64, 1024), F32),
            dma((4,)), dma((2,)), dma((8,)), dma((8,)), dma((3, 2, 5)), dma((3, 2, 5)),
            dma((8,)), dma((8,)), dma((8,)), dma((8,)), dma((8,)), dma((8,)), dma((8,)), dma((8,)),
            dma((4,)), dma((4,)), dma((4,)), dma((4,)), dma, dma,
        ],
        compiler_params=pltpu.CompilerParams(
            collective_id=0, has_side_effects=True, vmem_limit_bytes=62 * 1024 * 1024
        ),
        name="step",
    )(xv, xa, mods, bias, wqv, wqa, wov, woa)


def local(
    video_tokens, audio_tokens, qkv_video, out_video, qkv_audio, out_audio, gain_video, gain_audio,
    time_from, time_to, time_steps, windows, intersection,
):
    tokens = video_tokens.shape[1]
    vid = lax.axis_index("vid")
    blocks = tokens // BLK
    qpos = jnp.arange(tokens, dtype=jnp.int32)[:, None, None]
    kpos = (jnp.arange(3, dtype=jnp.int32)[:, None] - 1) * tokens + jnp.arange(tokens, dtype=jnp.int32)[None, :]
    kpos = kpos[None]
    at = vid * tokens + kpos
    inside = (at >= 0) & (at < lax.axis_size("vid") * tokens)
    near_by = jnp.abs(qpos - kpos)
    qblk = vid * blocks + qpos // BLK
    kblk = at // BLK
    padded = jnp.pad(intersection[0], ((blocks, blocks), (0, 0)))
    ranges = lax.dynamic_slice_in_dim(padded, vid * blocks, 3 * blocks, axis=0)
    low = jnp.broadcast_to(ranges[:, 0][:, None], (3 * blocks, BLK)).reshape(1, 3, tokens)
    high = jnp.broadcast_to(ranges[:, 1][:, None], (3 * blocks, BLK)).reshape(1, 3, tokens)
    low_q = low[0, 1][:, None, None]
    high_q = high[0, 1][:, None, None]
    vv = inside & (near_by < windows[0, 0])
    va = inside & (kblk >= low_q) & (kblk < high_q)
    av = inside & (qblk >= low) & (qblk < high)
    aa = inside & (near_by < windows[0, 1])
    admit = jnp.stack([jnp.stack([vv, va], 2), jnp.stack([av, aa], 2)], 0)
    bias = jnp.where(admit, 0.0, -1e30).astype(F32).reshape(2, tokens, 6 * tokens)

    now = time_steps[0, 0]
    stride = time_steps[0, 1]

    def row(table, index):
        return lax.dynamic_index_in_dim(table, index, 0, keepdims=False)

    gains = jnp.stack([gain_video, gain_audio])
    first = row(time_from, now) + row(time_to, now)
    student = row(time_from, now) + row(time_to, now - STEPS * stride)
    second = row(time_from, now - stride) + row(time_to, now - stride)
    conds = jnp.stack([first, student, second])
    mods = (gains[None] * (1.0 + conds[:, None, :])).reshape(6, -1)
    step = jnp.broadcast_to(-stride.astype(F32) / TGRID, (2, mods.shape[1]))
    mods = jnp.concatenate([mods, step], 0)
    d_video, d_audio, grads = fused(
        video_tokens[0], audio_tokens[0], mods, bias,
        qkv_video.reshape(2048, 768), qkv_audio.reshape(2048, 768),
        out_video.reshape(256, 2048), out_audio.reshape(256, 2048),
    )

    def split(m):
        return grads[m, :, :768].reshape(64, 2, 384), grads[m, :, 768:].T.reshape(2, 128, 64)

    qv, ov = split(0)
    qa, oa = split(1)
    return d_video[None], d_audio[None], qv, ov, qa, oa


def solution(mesh):
    return jax.shard_map(
        local,
        mesh=mesh,
        in_specs=(
            P("clip", "vid", None), P("clip", "vid", None), P(None, "aud", None), P("aud", None, None),
            P(None, "aud", None), P("aud", None, None), P(), P(), P(), P(),
            P("clip", None), P("clip", None), P("clip", None, None),
        ),
        out_specs=(
            P("clip", "vid", None), P("clip", "vid", None), P(("clip", "vid"), "aud", None),
            P("aud", None, ("clip", "vid")), P(("clip", "vid"), "aud", None), P("aud", None, ("clip", "vid")),
        ),
        check_vma=False,
    )
```

time: 894 us -> 189 us (0.21)
  the two profiles are of different devices: /device:TPU:1 before, /device:TPU:42 now
where the time goes in v1:
time: 189 us; the launch traced here: 188 us
  Pallas kernels  159 us (84%)
  local copies, waits for them, and re-layouts  19.3 us (10%)
  between operations  5.92 us (3%)
  other arithmetic  4.57 us (2%)
    pallas_call x1, Pallas kernels, fused(): pl.pallas_call(kernel, out_shape=(jax.ShapeDtypeStruct((128, 2048), BF16)...  159 us
    unnamed x9, local copies, waits for them, and re-layouts  10.3 us

profile of v1, /device:TPU:42, one launch (start us, length us, event | category | flops | bytes accessed | tf_op | source)
XLA Modules:
  0.0 188.3 jit_solution(6538356576118456783)
XLA Ops:
  0.7 0.1 compare_and_fusion.2
  0.7 0.8 constant_dynamic-slice_fusion
  1.5 1.3 fusion.9
  8.0 1.3 fusion.8
  9.3 0.1 broadcast_in_dim.43
  9.4 0.1 broadcast_in_dim.46
  9.5 0.1 add_select_fusion.1
  9.6 0.1 broadcast_in_dim.47
  9.6 0.1 broadcast_in_dim.50
  9.7 0.1 broadcast_in_dim.48
  9.8 0.1 broadcast_in_dim.44
  9.9 0.1 broadcast_in_dim.49
  10.0 0.1 broadcast_in_dim.45
  10.1 0.7 pad_maximum_fusion
  10.8 1.0 dynamic-slice_add_fusion.2
  11.9 0.6 concatenate.8.mods
  12.6 1.6 fusion.2
  14.2 0.2 copy.21
  14.4 0.2 copy.22
  14.6 1.0 add_select_fusion.bias
  15.6 4.3 %copy.27 = bf16[256,8,2,384]{3,1,2,0:T(8,128)(2,1)} copy(bf16[256,8,2,384]{3,2,1,0:T(2,128)(2,1)} %bitcast.41) | data formatting | bytes 6291456
  19.9 0.0 copy-done
  19.9 2.3 %copy.28 = bf16[256,8,2,384]{3,1,2,0:T(8,128)(2,1)} copy(bf16[256,8,2,384]{3,2,1,0:T(2,128)(2,1)S(1)} %bitcast.42) | data formatting | bytes 6291456
  22.3 158.5 %step.1 = (bf16[128,2048]{1,0:T(8,128)(2,1)}, bf16[128,2048]{1,0:T(8,128)(2,1)}, f32[2,64,1024]{2,1,0:T(8,128)}) custom-call(bf16[128,2048]{1,0:T(8,128)(2,1)} %bitcast.45, bf16[128,2048]{1,0:T(8,128)(2,1)} %bitcast.46, f32[8,2048]{1,0:T(8,128)} %concatenate.8.mods, f32[2,128,768]{2,1,0:T(8,128)} %add_select_fusion.bias, bf16[2048,768]{1,0:T(8,128)(2,1)} %bitcast.39, ...), custom_call_target="tpu_custom_call" | custom-call | tf_op jit(solution)/shard_map/step/pallas_call | solution.py:387
  180.8 0.9 slice_bitcast_fusion
  181.8 1.1 fusion.7
  182.8 0.8 reshape_squeeze.7
  183.6 0.6 copy.31
  184.2 0.6 copy.32
  184.9 0.8 reshape_squeeze.6
  185.6 1.9 copy.35
  187.5 0.8 copy.36
  (12 shorter events, 0.2 us)
Async XLA Ops:
  15.6 4.3 %copy-start = (bf16[2048,2,384]{2,1,0:T(2,128)(2,1)S(1)}, bf16[2048,2,384]{2,1,0:T(2,128)(2,1)}, u32[]{:S(2)}) copy-start(bf16[2048,2,384]{2,1,0:T(2,128)(2,1)} %param.17) | copy-start | bytes 9437188
  180.8 6.7 %copy-start.1 = (bf16[128,2048]{1,0:T(8,128)(2,1)S(1)}, bf16[128,2048]{1,0:T(8,128)(2,1)}, u32[]{:S(2)}) copy-start(bf16[128,2048]{1,0:T(8,128)(2,1)} %get-tuple-element.10) | copy-start | bytes 1572868

commit v2 on v1

v2 whole, which is shorter than its diff:
```python
import jax
import jax.numpy as jnp
from jax import lax
from jax.experimental import pallas as pl
from jax.experimental.pallas import tpu as pltpu
from jax.sharding import PartitionSpec as P

BLK = 32
TGRID = 64
STEPS = 2
EPSILON = 1e-06
MESH = pl.DeviceIdType.MESH
F32 = jnp.float32
BF16 = jnp.bfloat16
NT = (((1,), (1,)), ((), ()))
TN = (((0,), (0,)), ((), ()))
NN = (((1,), (0,)), ((), ()))
T1, ST, T2 = 0, 1, 2
VMEM_LIMIT = 62 * 1024 * 1024


def dot(a, b, dims):
    return lax.dot_general(a, b, dims, preferred_element_type=F32)


def kernel(
    steps, windows, ranges, xv, xa, gv, ga, tf, tt, wqv, wqa, wov, woa,
    dv_out, da_out, qv_out, qa_out, ov_out, oa_out,
    WQ, WO, N0, NS, NG, NGT, OB, OG, GS, GG, DQ, DQS, DKVS, DGQ, DGK, QR, KV, PS, ACC,
    SB, R1, S2, R2, ZS, ZR, AG, DIFF, DO, DKV, DKS, DKR,
    WA, RA, WB, RB, WC, RC, MODS, BIAS,
    w_sem, o_sem, kv_s, kv_r, ar_s, ar_r, ng_s, ng_r, og_s, og_r, gg_s, gg_r,
    dq_s, dq_r, dk_s, dk_r, wa_s, wa_r, wb_s, wb_r, wc_s, wc_r,
):
    v = lax.axis_index("vid")
    a = lax.axis_index("aud")
    c = lax.axis_index("clip")
    core = lax.rem(v, 2)
    yy = v // 2
    x = a // 2
    zh = lax.rem(a, 2)
    b0 = lax.rem(x, 2)
    b1 = x // 2
    q = lax.rem(b0 + b1, 2)
    near = (x + 1 - 2 * b0) * 2 + zh
    far = (3 - x) * 2 + zh
    across = a + 1 - 2 * zh
    first = (near, far)
    second = (far, near)
    keep1 = (q, b1)
    keep2 = (b1, b0)
    keepf = (b1, 1 - b0)
    right = lax.rem(v + 1, 8)
    left = lax.rem(v + 7, 8)
    y_near = yy + 1 - 2 * lax.rem(yy, 2)
    y_far = 3 - yy
    y_one = (1 - core) * y_near + core * y_far
    y_two = core * y_near + (1 - core) * y_far
    y_last = 6 - yy - y_one - y_two
    mate = v + 1 - 2 * core

    def rows(value):
        return pl.ds(pl.multiple_of(value, 16), 16)

    chunks = [(g, m) for g in range(2) for m in range(2)]
    own, other, give, hold = {}, {}, {}, {}
    for g, m in chunks:
        base = 64 * g + 32 * keep1[m]
        away = 64 * g + 32 * (1 - keep1[m])
        own[g, m] = rows(base + 16 * keep2[m])
        other[g, m] = rows(base + 16 * (1 - keep2[m]))
        give[g, m] = rows(away + 16 * (1 - keepf[m]))
        hold[g, m] = rows(away + 16 * keepf[m])

    loads = [
        pltpu.make_async_copy(wqv, WQ.at[0], w_sem.at[0]),
        pltpu.make_async_copy(wqa, WQ.at[1], w_sem.at[1]),
        pltpu.make_async_copy(wov, WO.at[0], w_sem.at[2]),
        pltpu.make_async_copy(woa, WO.at[1], w_sem.at[3]),
    ]
    for load in loads:
        load.start()

    barrier = pltpu.get_barrier_semaphore()
    greet = [{"vid": lax.rem(v + d, 8)} for d in range(1, 8)]
    greet += [{"aud": peer} for peer in (near, far, across)]
    greet += [{"clip": lax.rem(c + d, 4), "vid": 2 * yy + k} for d in range(1, 4) for k in range(2)]
    for peer in greet:
        pl.semaphore_signal(barrier, 1, device_id=peer, device_id_type=MESH)

    pending = []

    def remote(src, dst, send, recv, device):
        return pltpu.make_async_remote_copy(
            src_ref=src, dst_ref=dst, send_sem=send, recv_sem=recv, device_id=device, device_id_type=MESH
        )

    def go(copy):
        copy.start()
        pending.append(copy)

    def wide(ref):
        return ref.astype(F32)

    now = steps[0, 0]
    stride = steps[0, 1]
    step = -stride.astype(F32) / TGRID
    conds = (
        tf[pl.ds(now, 1), :] + tt[pl.ds(now, 1), :],
        tf[pl.ds(now, 1), :] + tt[pl.ds(now - STEPS * stride, 1), :],
        tf[pl.ds(now - stride, 1), :] + tt[pl.ds(now - stride, 1), :],
    )
    gains = (gv, ga)
    for net in range(3):
        for m in range(2):
            MODS[2 * net + m : 2 * net + m + 1, :] = gains[m][...] * (1.0 + conds[net])

    xs = (xv, xa)

    def normed(net, m, r):
        part = pl.ds(pl.multiple_of(r * 32, 32), 32)
        cur = wide(xs[m][part, :])
        inv = lax.rsqrt(jnp.mean(cur * cur, -1, keepdims=True) + EPSILON)
        out = (cur * inv * MODS[2 * net + m : 2 * net + m + 1, :]).astype(BF16)
        N0[net, m, part, :] = out
        return part, out

    def store_qkv(net, m, value):
        rounded = value.astype(BF16)
        for h in range(2):
            QR[net, m, :, 128 * h : 128 * h + 128] = rounded[:, 384 * h : 384 * h + 128]
            KV[net, 1, m, :, 256 * h : 256 * h + 256] = rounded[:, 384 * h + 128 : 384 * h + 384]

    def kv_copies(net):
        return (
            remote(KV.at[net, 1], KV.at[net, 0], kv_s.at[2 * net], kv_r.at[2 * net], {"vid": right}),
            remote(KV.at[net, 1], KV.at[net, 2], kv_s.at[2 * net + 1], kv_r.at[2 * net + 1], {"vid": left}),
        )

    def kv_start(net):
        for copy in kv_copies(net):
            go(copy)

    def kv_wait(net):
        for copy in kv_copies(net):
            copy.wait_recv()

    for m in range(2):

        def norm_teacher(r, carry, m=m):
            normed(T1, m, r)
            return carry

        lax.fori_loop(0, 4, norm_teacher, 0)
    for m in range(2):
        loads[m].wait()
        store_qkv(T1, m, dot(N0[T1, m], WQ[m], NN))
    pl.semaphore_wait(barrier, len(greet))
    kv_start(T1)

    for m in range(2):

        def norm_student(r, carry, m=m):
            part, student = normed(ST, m, r)
            for s in range(16):
                NS[m, s // 4, s % 4, part, :] = student[:, 128 * s : 128 * s + 128]
            return carry

        lax.fori_loop(0, 4, norm_student, 0)
        store_qkv(ST, m, dot(N0[ST, m], WQ[m], NN))
    kv_start(ST)

    qpos = lax.broadcasted_iota(jnp.int32, (128, 128), 0)
    kpos = lax.broadcasted_iota(jnp.int32, (128, 128), 1)
    qblk = lax.broadcasted_iota(jnp.int32, (128, 1), 0) // BLK
    kblk = lax.broadcasted_iota(jnp.int32, (1, 128), 1) // BLK

    def spans(which, first_block, block_of):
        out = jnp.zeros(block_of.shape, jnp.int32)
        for i in range(4):
            at = jnp.clip(first_block + i, 0, 31)
            out = jnp.where(block_of == i, ranges[0, at, which], out)
        return out

    low_q = spans(0, 4 * v, qblk)
    high_q = spans(1, 4 * v, qblk)
    for slot in range(3):
        shard = v + slot - 1
        at = kpos + 128 * shard
        inside = (at >= 0) & (at < 1024)
        apart = jnp.abs(qpos - (kpos + 128 * (slot - 1)))
        keys_at = kblk + 4 * shard
        low_k = spans(0, 4 * shard, kblk)
        high_k = spans(1, 4 * shard, kblk)
        query_at = qblk + 4 * v
        tests = (
            (apart < windows[0, 0], (keys_at >= low_q) & (keys_at < high_q)),
            ((query_at >= low_k) & (query_at < high_k), apart < windows[0, 1]),
        )
        for m in range(2):
            for k in range(2):
                cols = slice(256 * slot + 128 * k, 256 * slot + 128 * k + 128)
                BIAS[m, :, cols] = jnp.where(inside & tests[m][k], 0.0, -1e30)

    def spread(src, dst, send, recv, offsets):
        for d in offsets:
            peer = 2 * lax.rem(yy + d[0], 4) + lax.rem(core + d[1], 2)
            go(remote(src(lax.rem(peer, 2), peer // 2), dst.at[v], send.at[peer], recv.at[v], {"vid": peer}))

    def collect(dst, send, recv):
        for d in range(1, 8):
            peer = lax.rem(v + d, 8)
            remote(dst.at[peer], dst.at[peer], send.at[peer], recv.at[peer], {"vid": peer}).wait_recv()

    close = [(0, 1), (1, 0), (3, 0), (1, 1), (3, 1)]
    distant = [(2, 0), (2, 1)]

    factor = 128 ** (-0.5)

    def attention(net, m, save):
        for h in range(2):
            queries = QR[net, m, :, 128 * h : 128 * h + 128]
            keys = KV[net, :, :, :, 256 * h : 256 * h + 128].reshape(768, 128)
            values = KV[net, :, :, :, 256 * h + 128 : 256 * h + 256].reshape(768, 128)
            scores = dot(queries, keys, NT) * factor + BIAS[m]
            shifted = jnp.exp(scores - jnp.max(scores, -1, keepdims=True))
            prob = shifted * (1.0 / jnp.sum(shifted, -1, keepdims=True))
            if save:
                PS[2 * m + h] = prob
            OB[net, m, :, 128 * h : 128 * h + 128] = dot(prob.astype(BF16), values, NN).astype(BF16)

    def project_out(net, m):
        return dot(OB[net, m], WO[m], NN)

    def aud(i, g, m, kind, src, dst, device):
        return remote(src, dst, ar_s.at[i, g, m, kind], ar_r.at[i, g, m, kind], {"aud": device})

    def sum_start(i, m):
        for kind, part in ((0, give), (1, hold)):
            for g in range(2):
                go(aud(i, g, m, kind, SB.at[i, m, part[g, m]], R1.at[i, g, m, kind], first[m]))

    def sum_1(i):
        for g, m in chunks:
            aud(i, g, m, 0, R1.at[i, g, m, 0], R1.at[i, g, m, 0], first[m]).wait_recv()
            S2[i, g, m] = (wide(SB[i, m, other[g, m], :]) + wide(R1[i, g, m, 0])).astype(BF16)
            go(aud(i, g, m, 2, S2.at[i, g, m], R2.at[i, g, m], second[m]))

    def sum_2(i):
        for g, m in chunks:
            aud(i, g, m, 1, R1.at[i, g, m, 1], R1.at[i, g, m, 1], first[m]).wait_recv()
            aud(i, g, m, 2, R2.at[i, g, m], R2.at[i, g, m], second[m]).wait_recv()
            ZS[i, g, m] = (
                wide(SB[i, m, own[g, m], :]) + wide(R1[i, g, m, 1]) + wide(R2[i, g, m])
            ).astype(BF16)
            go(aud(i, g, m, 3, ZS.at[i, g, m], ZR.at[i, g, m], across))

    def summed(i, g, m):
        aud(i, g, m, 3, ZR.at[i, g, m], ZR.at[i, g, m], across).wait_recv()
        return wide(ZS[i, g, m]) + wide(ZR[i, g, m])

    def share(i, g, m, value):
        AG[i, m, own[g, m], :] = value.astype(BF16)
        part = AG.at[i, m, own[g, m]]
        go(aud(i, g, m, 4, part, part, second[m]))
        go(aud(i, g, m, 5, part, part, first[m]))

    def share_on(i):
        for g, m in chunks:
            part = AG.at[i, m, other[g, m]]
            aud(i, g, m, 4, part, part, second[m]).wait_recv()
            go(aud(i, g, m, 6, part, part, first[m]))

    def share_end(i):
        for g, m in chunks:
            part = AG.at[i, m, hold[g, m]]
            aud(i, g, m, 5, part, part, first[m]).wait_recv()
            part = AG.at[i, m, give[g, m]]
            aud(i, g, m, 6, part, part, first[m]).wait_recv()

    for m in range(2):
        loads[2 + m].wait()
    kv_wait(T1)
    for m in range(2):
        attention(T1, m, False)
        field = project_out(T1, m)
        SB[0, m] = field.astype(BF16)
        ACC[m] = -field
        sum_start(0, m)
    kv_wait(ST)
    NG[v] = NS[core, :, yy]
    spread(lambda k, y: NS.at[k, :, y], NG, ng_s, ng_r, close + distant)
    attention(ST, 0, True)
    sum_1(0)
    attention(ST, 1, True)
    OG[v] = OB[ST, core]
    spread(lambda k, y: OB.at[ST, k], OG, og_s, og_r, close + distant)
    sum_2(0)
    for m in range(2):
        ACC[m] = ACC[m] + 2.0 * project_out(ST, m)
    for g, m in chunks:
        cur = wide(xs[m][own[g, m], :]) + step * summed(0, g, m)
        inv = lax.rsqrt(jnp.mean(cur * cur, -1, keepdims=True) + EPSILON)
        share(0, g, m, cur * inv * MODS[4 + m : 5 + m, :])
    share_on(0)
    share_end(0)

    for m in range(2):
        store_qkv(T2, m, dot(AG[0, m], WQ[m], NN))
    kv_start(T2)
    kv_wait(T2)
    for m in range(2):
        attention(T2, m, False)
        SB[1, m] = (ACC[m] - project_out(T2, m)).astype(BF16)
        sum_start(1, m)
    collect(NG, ng_s, ng_r)
    for s in range(4):
        NGT[128 * s : 128 * s + 128, :] = NG[:, s].reshape(1024, 128).T
    sum_1(1)
    collect(OG, og_s, og_r)
    sum_2(1)
    for g, m in chunks:
        diff = step * summed(1, g, m)
        DIFF[g, m] = diff
        share(1, g, m, 2.0 * step * diff)
    share_on(1)
    share_end(1)

    for m in range(2):
        for s in range(16):
            GS[m, s // 4, s % 4] = AG[1, m, :, 128 * s : 128 * s + 128]
    GG[v] = GS[core, :, yy]
    spread(lambda k, y: GS.at[k, :, y], GG, gg_s, gg_r, close)
    for m in range(2):
        DO[m] = dot(AG[1, m], WO[m], NT).astype(BF16)
    for m in range(2):
        for h in range(2):
            cols = slice(256 * h, 256 * h + 128)
            vcols = slice(256 * h + 128, 256 * h + 256)
            queries = QR[ST, m, :, 128 * h : 128 * h + 128]
            keys = KV[ST, :, :, :, cols].reshape(768, 128)
            values = KV[ST, :, :, :, vcols].reshape(768, 128)
            grad_out = DO[m, :, 128 * h : 128 * h + 128]
            prob = PS[2 * m + h]
            grad_prob = dot(grad_out, values, NT)
            center = jnp.sum(prob * grad_prob, -1, keepdims=True)
            dscore = (prob * (grad_prob - center) * factor).astype(BF16)
            dquery = dot(dscore, keys, NN).astype(BF16)
            DQ[m, :, 384 * h : 384 * h + 128] = dquery
            DQS[m, :, 128 * h : 128 * h + 128] = dquery
            dkey = dot(dscore, queries, TN).reshape(3, 2, 128, 128)
            dvalue = dot(prob.astype(BF16), grad_out, TN).reshape(3, 2, 128, 128)
            if m == 0:
                DKV[:, :, :, cols] = dkey
                DKV[:, :, :, vcols] = dvalue
            else:
                DKV[:, :, :, cols] = DKV[:, :, :, cols] + dkey
                DKV[:, :, :, vcols] = DKV[:, :, :, vcols] + dvalue
    DKS[0] = DKV[0].astype(BF16)
    DKS[1] = DKV[2].astype(BF16)
    edges = (
        remote(DKS.at[0], DKR.at[0], kv_s.at[6], kv_r.at[6], {"vid": left}),
        remote(DKS.at[1], DKR.at[1], kv_s.at[7], kv_r.at[7], {"vid": right}),
    )
    for copy in edges:
        go(copy)

    def line_start(src, dst, s_sem, r_sem):
        dst[yy, core] = src[core]
        go(remote(src.at[1 - core], dst.at[yy, core], s_sem.at[0], r_sem.at[0], {"vid": mate}))

    def line_send(dst, s_sem, r_sem):
        part = dst.at[yy, 1 - core]
        remote(part, part, s_sem.at[0], r_sem.at[0], {"vid": mate}).wait_recv()
        part = dst.at[yy]
        go(remote(part, part, s_sem.at[1], r_sem.at[1], {"vid": 2 * y_one + core}))
        go(remote(part, part, s_sem.at[2], r_sem.at[2], {"vid": 2 * y_two + core}))

    def line_on(dst, s_sem, r_sem):
        part = dst.at[y_one]
        remote(part, part, s_sem.at[1], r_sem.at[1], {"vid": 2 * y_one + core}).wait_recv()
        go(remote(part, part, s_sem.at[3], r_sem.at[3], {"vid": 2 * y_two + core}))

    def line_end(dst, s_sem, r_sem):
        part = dst.at[y_two]
        remote(part, part, s_sem.at[2], r_sem.at[2], {"vid": 2 * y_two + core}).wait_recv()
        part = dst.at[y_last]
        remote(part, part, s_sem.at[3], r_sem.at[3], {"vid": 2 * y_two + core}).wait_recv()

    line_start(DQS, DGQ, dq_s, dq_r)
    line_send(DGQ, dq_s, dq_r)
    for copy in edges:
        copy.wait_recv()
    for m in range(2):
        owned = (DKV[1, m] + wide(DKR[0, m]) + wide(DKR[1, m])).astype(BF16)
        DKVS[m] = owned
        for h in range(2):
            DQ[m, :, 384 * h + 128 : 384 * h + 384] = owned[:, 256 * h : 256 * h + 256]
    line_start(DKVS, DGK, dk_s, dk_r)
    SB[2, 0] = dot(DQ[0], WQ[0], NT).astype(BF16)
    sum_start(2, 0)
    line_send(DGK, dk_s, dk_r)
    SB[2, 1] = dot(DQ[1], WQ[1], NT).astype(BF16)
    sum_start(2, 1)
    line_on(DGQ, dq_s, dq_r)
    spread(lambda k, y: GS.at[k, :, y], GG, gg_s, gg_r, distant)

    def clip_start(send, got, s_sem, r_sem):
        for d in range(4):
            peer = lax.rem(c + d, 4)
            for k in range(2):
                to = lax.rem(core + 1 - k, 2)
                half = pl.ds(pl.multiple_of(64 * to, 64), 64)
                if d == 0 and k == 1:
                    got[core, c] = send[c, half, :]
                else:
                    device = {"clip": peer, "vid": 2 * yy + to}
                    go(remote(send.at[peer, half], got.at[core, c], s_sem.at[to, peer], r_sem.at[core, c], device))

    def clip_end(got, s_sem, r_sem):
        for d in range(4):
            peer = lax.rem(c + d, 4)
            for k in range(2):
                if d == 0 and k == 1:
                    continue
                to = lax.rem(core + 1 - k, 2)
                part = got.at[to, peer]
                device = {"clip": peer, "vid": 2 * yy + to}
                remote(part, part, s_sem.at[to, peer], r_sem.at[to, peer], device).wait_recv()

    def clip_sum(got, m):
        return (wide(got[m, 0]) + wide(got[m, 1])) + (wide(got[m, 2]) + wide(got[m, 3]))

    sum_1(2)
    line_on(DGK, dk_s, dk_r)
    line_end(DGQ, dq_s, dq_r)
    dq_all = DGQ[...].reshape(1024, 256)
    WA[...] = dot(NGT[...], dq_all, NN).astype(BF16).reshape(4, 128, 256)
    clip_start(WA, RA, wa_s, wa_r)
    sum_2(2)
    line_end(DGK, dk_s, dk_r)
    dk_all = DGK[...].reshape(1024, 512)
    WB[...] = dot(NGT[...], dk_all, NN).astype(BF16).reshape(4, 128, 512)
    clip_start(WB, RB, wb_s, wb_r)
    for g, m in chunks:
        cur = wide(xs[m][own[g, m], :])
        inv = lax.rsqrt(jnp.mean(cur * cur, -1, keepdims=True) + EPSILON)
        scaled = summed(2, g, m) * MODS[2 + m : 3 + m, :]
        back = inv * scaled - cur * (inv * inv * inv) * jnp.mean(scaled * cur, -1, keepdims=True)
        share(2, g, m, DIFF[g, m] + back)
    collect(GG, gg_s, gg_r)
    o_all = OG[...].reshape(1024, 256)
    for s in range(4):
        WC[s] = dot(GG[:, s].reshape(1024, 128), o_all, TN).astype(BF16)
    clip_start(WC, RC, wc_s, wc_r)
    share_on(2)
    q_outs = (qv_out, qa_out)
    o_outs = (ov_out, oa_out)
    clip_end(RA, wa_s, wa_r)
    for m in range(2):
        total = clip_sum(RA, m)
        for h in range(2):
            q_outs[m][:, h, 0:128] = total[:, 128 * h : 128 * h + 128]
    share_end(2)
    outs = (
        pltpu.make_async_copy(AG.at[2, 0], dv_out, o_sem.at[0]),
        pltpu.make_async_copy(AG.at[2, 1], da_out, o_sem.at[1]),
    )
    for copy in outs:
        copy.start()
    clip_end(RB, wb_s, wb_r)
    for m in range(2):
        total = clip_sum(RB, m)
        for h in range(2):
            q_outs[m][:, h, 128:384] = total[:, 256 * h : 256 * h + 256]
    clip_end(RC, wc_s, wc_r)
    for m in range(2):
        total = clip_sum(RC, m)
        for h in range(2):
            o_outs[m][h] = total[:, 128 * h : 128 * h + 128]
    for copy in outs:
        copy.wait()
    for copy in pending:
        copy.wait_send()


def vm(shape, kind=BF16):
    return pltpu.VMEM(shape, kind)


def fused(*operands):
    dma = pltpu.SemaphoreType.DMA
    inside = pl.BlockSpec(memory_space=pltpu.VMEM)
    scalar = pl.BlockSpec(memory_space=pltpu.SMEM)
    outside = pl.BlockSpec(memory_space=pl.ANY)
    shape = jax.ShapeDtypeStruct
    return pl.pallas_call(
        kernel,
        out_shape=(
            shape((128, 2048), BF16), shape((128, 2048), BF16), shape((64, 2, 384), F32),
            shape((64, 2, 384), F32), shape((2, 64, 128), F32), shape((2, 64, 128), F32),
        ),
        in_specs=[scalar] * 3 + [inside] * 6 + [outside] * 4,
        out_specs=(outside, outside, inside, inside, inside, inside),
        scratch_shapes=[
            vm((2, 2048, 768)), vm((2, 256, 2048)), vm((2, 2, 128, 2048)), vm((2, 4, 4, 128, 128)),
            vm((8, 4, 128, 128)), vm((512, 1024)), vm((3, 2, 128, 256)), vm((8, 128, 256)),
            vm((2, 4, 4, 128, 128)), vm((8, 4, 128, 128)), vm((2, 128, 768)), vm((2, 128, 256)),
            vm((2, 128, 512)), vm((4, 2, 128, 256)), vm((4, 2, 128, 512)), vm((3, 2, 128, 256)),
            vm((3, 3, 2, 128, 512)), vm((4, 128, 768), F32), vm((2, 128, 2048), F32),
            vm((3, 2, 128, 2048)), vm((3, 2, 2, 2, 16, 2048)), vm((3, 2, 2, 16, 2048)),
            vm((3, 2, 2, 16, 2048)), vm((3, 2, 2, 16, 2048)), vm((3, 2, 2, 16, 2048)),
            vm((3, 2, 128, 2048)), vm((2, 2, 16, 2048), F32), vm((2, 128, 256)),
            vm((3, 2, 128, 512), F32), vm((2, 2, 128, 512)), vm((2, 2, 128, 512)),
            vm((4, 128, 256)), vm((2, 4, 64, 256)), vm((4, 128, 512)), vm((2, 4, 64, 512)),
            vm((4, 128, 256)), vm((2, 4, 64, 256)), vm((8, 2048), F32), vm((2, 128, 768), F32),
            dma((4,)), dma((2,)), dma((8,)), dma((8,)), dma((3, 2, 2, 7)), dma((3, 2, 2, 7)),
            dma((8,)), dma((8,)), dma((8,)), dma((8,)), dma((8,)), dma((8,)),
            dma((4,)), dma((4,)), dma((4,)), dma((4,)),
            dma((2, 4)), dma((2, 4)), dma((2, 4)), dma((2, 4)), dma((2, 4)), dma((2, 4)),
        ],
        compiler_params=pltpu.CompilerParams(
            collective_id=0, has_side_effects=True, vmem_limit_bytes=VMEM_LIMIT
        ),
        name="step",
    )(*operands)


def local(
    video_tokens, audio_tokens, qkv_video, out_video, qkv_audio, out_audio, gain_video, gain_audio,
    time_from, time_to, time_steps, windows, intersection,
):
    d_video, d_audio, qv, qa, ov, oa = fused(
        time_steps, windows, intersection, video_tokens[0], audio_tokens[0],
        gain_video.reshape(1, 2048), gain_audio.reshape(1, 2048), time_from, time_to,
        qkv_video.reshape(2048, 768), qkv_audio.reshape(2048, 768),
        out_video.reshape(256, 2048), out_audio.reshape(256, 2048),
    )
    return d_video[None], d_audio[None], qv, ov.swapaxes(1, 2), qa, oa.swapaxes(1, 2)


def solution(mesh):
    return jax.shard_map(
        local,
        mesh=mesh,
        in_specs=(
            P("clip", "vid", None), P("clip", "vid", None), P(None, "aud", None), P("aud", None, None),
            P(None, "aud", None), P("aud", None, None), P(), P(), P(), P(),
            P("clip", None), P("clip", None), P("clip", None, None),
        ),
        out_specs=(
            P("clip", "vid", None), P("clip", "vid", None), P(("clip", "vid"), "aud", None),
            P("aud", None, ("clip", "vid")), P(("clip", "vid"), "aud", None), P("aud", None, ("clip", "vid")),
        ),
        check_vma=False,
    )
```

time: 189 us -> 167 us (0.88)
  the two profiles are of different devices: /device:TPU:42 before, /device:TPU:232 now
where the time goes in v2:
time: 167 us
  Pallas kernels  148 us (89%)
  local copies, waits for them, and re-layouts  18 us (11%)
    pallas_call x1, Pallas kernels, fused(): pl.pallas_call(kernel, out_shape=(shape((128, 2048), BF16), shape((128, 2...  148 us
    unnamed x11, local copies, waits for them, and re-layouts  18 us

profile of v2, /device:TPU:232, one launch (start us, length us, event | category | flops | bytes accessed | tf_op | source)
XLA Modules:
  0.0 166.9 jit_solution(3507548637943921654)
XLA Ops:
  0.6 1.4 copy.19.ranges
  2.0 0.0 copy-start
  2.0 4.3 %copy.20 = bf16[256,8,2,384]{3,1,2,0:T(8,128)(2,1)} copy(bf16[256,8,2,384]{3,2,1,0:T(2,128)(2,1)} %bitcast.16) | data formatting | bytes 6291456
  6.3 0.0 copy-done
  6.3 2.3 %copy.21 = bf16[256,8,2,384]{3,1,2,0:T(8,128)(2,1)} copy(bf16[256,8,2,384]{3,2,1,0:T(2,128)(2,1)S(1)} %bitcast.17) | data formatting | bytes 6291456
  8.7 148.2 %step.1 = (bf16[128,2048]{1,0:T(8,128)(2,1)}, bf16[128,2048]{1,0:T(8,128)(2,1)}, f32[64,2,384]{2,1,0:T(2,128)}, f32[64,2,384]{2,1,0:T(2,128)}, f32[2,64,128]{2,1,0:T(8,128)}, /*index=5*/f32[2,64,128]{2,1,0:T(8,128)}) custom-call(s32[1,2]{1,0:T(1,128)} %steps.1, s32[1,2]{1,0:T(1,128)} %windows.1, s32[1,32,2]{2,1,0:T(8,128)} %copy.19.ranges, ...), custom_call_target="tpu_custom_call" | custom-call | tf_op jit(solution)/shard_map/step/pallas_call | solution.py:497
  156.9 1.9 %copy.28 = bf16[1,128,2048]{2,1,0:T(8,128)(2,1)} copy(bf16[1,128,2048]{2,1,0:T(8,128)(2,1)} %bitcast.23) | data formatting | bytes 1048576
  158.8 1.9 %copy.29 = bf16[1,128,2048]{2,1,0:T(8,128)(2,1)} copy(bf16[1,128,2048]{2,1,0:T(8,128)(2,1)} %bitcast.22) | data formatting | bytes 1048576
  160.6 1.6 copy.30
  162.3 1.5 copy.31
  163.8 1.6 copy.32
  165.4 1.5 copy.33
Async XLA Ops:
  2.0 4.3 %copy-start = (bf16[2048,2,384]{2,1,0:T(2,128)(2,1)S(1)}, bf16[2048,2,384]{2,1,0:T(2,128)(2,1)}, u32[]{:S(2)}) copy-start(bf16[2048,2,384]{2,1,0:T(2,128)(2,1)} %param.17) | copy-start | bytes 9437188

commit v3 on v2

--- a/solution.py
+++ b/solution.py
@@ -26,11 +26,11 @@
 def kernel(
     steps, windows, ranges, xv, xa, gv, ga, tf, tt, wqv, wqa, wov, woa,
     dv_out, da_out, qv_out, qa_out, ov_out, oa_out,
-    WQ, WO, N0, NS, NG, NGT, OB, OG, GS, GG, DQ, DQS, DKVS, DGQ, DGK, QR, KV, PS, ACC,
+    WQ, WO, N0, NS, NG, NGT, OB, OG, GS, GG, DQ, DQS, DG, QR, KV, PS, ACC,
     SB, R1, S2, R2, ZS, ZR, AG, DIFF, DO, DKV, DKS, DKR,
-    WA, RA, WB, RB, WC, RC, MODS, BIAS,
+    W, WR, WS, WF, MODS, BIAS,
     w_sem, o_sem, kv_s, kv_r, ar_s, ar_r, ng_s, ng_r, og_s, og_r, gg_s, gg_r,
-    dq_s, dq_r, dk_s, dk_r, wa_s, wa_r, wb_s, wb_r, wc_s, wc_r,
+    dg_s, dg_r, cl_s, cl_r, wf_r,
 ):
     v = lax.axis_index("vid")
     a = lax.axis_index("aud")
@@ -84,7 +84,8 @@
     barrier = pltpu.get_barrier_semaphore()
     greet = [{"vid": lax.rem(v + d, 8)} for d in range(1, 8)]
     greet += [{"aud": peer} for peer in (near, far, across)]
-    greet += [{"clip": lax.rem(c + d, 4), "vid": 2 * yy + k} for d in range(1, 4) for k in range(2)]
+    greet += [{"clip": c + 1 - 2 * lax.rem(c, 2)}]
+    greet += [{"clip": lax.rem(c + 2, 4), "vid": 2 * yy + k} for k in range(2)]
     for peer in greet:
         pl.semaphore_signal(barrier, 1, device_id=peer, device_id_type=MESH)
 
@@ -179,7 +180,7 @@
         out = jnp.zeros(block_of.shape, jnp.int32)
         for i in range(4):
             at = jnp.clip(first_block + i, 0, 31)
-            out = jnp.where(block_of == i, ranges[0, at, which], out)
+            out = jnp.where(block_of == i, ranges[0, which, at], out)
         return out
 
     low_q = spans(0, 4 * v, qblk)
@@ -347,7 +348,7 @@
             dscore = (prob * (grad_prob - center) * factor).astype(BF16)
             dquery = dot(dscore, keys, NN).astype(BF16)
             DQ[m, :, 384 * h : 384 * h + 128] = dquery
-            DQS[m, :, 128 * h : 128 * h + 128] = dquery
+            DQS[0, m, :, 128 * h : 128 * h + 128] = dquery
             dkey = dot(dscore, queries, TN).reshape(3, 2, 128, 128)
             dvalue = dot(prob.astype(BF16), grad_out, TN).reshape(3, 2, 128, 128)
             if m == 0:
@@ -365,117 +366,121 @@
     for copy in edges:
         go(copy)
 
-    def line_start(src, dst, s_sem, r_sem):
-        dst[yy, core] = src[core]
-        go(remote(src.at[1 - core], dst.at[yy, core], s_sem.at[0], r_sem.at[0], {"vid": mate}))
-
-    def line_send(dst, s_sem, r_sem):
-        part = dst.at[yy, 1 - core]
-        remote(part, part, s_sem.at[0], r_sem.at[0], {"vid": mate}).wait_recv()
-        part = dst.at[yy]
-        go(remote(part, part, s_sem.at[1], r_sem.at[1], {"vid": 2 * y_one + core}))
-        go(remote(part, part, s_sem.at[2], r_sem.at[2], {"vid": 2 * y_two + core}))
-
-    def line_on(dst, s_sem, r_sem):
-        part = dst.at[y_one]
-        remote(part, part, s_sem.at[1], r_sem.at[1], {"vid": 2 * y_one + core}).wait_recv()
-        go(remote(part, part, s_sem.at[3], r_sem.at[3], {"vid": 2 * y_two + core}))
-
-    def line_end(dst, s_sem, r_sem):
-        part = dst.at[y_two]
-        remote(part, part, s_sem.at[2], r_sem.at[2], {"vid": 2 * y_two + core}).wait_recv()
-        part = dst.at[y_last]
-        remote(part, part, s_sem.at[3], r_sem.at[3], {"vid": 2 * y_two + core}).wait_recv()
-
-    line_start(DQS, DGQ, dq_s, dq_r)
-    line_send(DGQ, dq_s, dq_r)
+    def line(n, k, part, device):
+        return remote(part, part, dg_s.at[n, k], dg_r.at[n, k], {"vid": device})
+
+    def line_start(n):
+        DG[n, yy, core] = DQS[n, core]
+        go(remote(DQS.at[n, 1 - core], DG.at[n, yy, core], dg_s.at[n, 0], dg_r.at[n, 0], {"vid": mate}))
+
+    def line_send(n):
+        line(n, 0, DG.at[n, yy, 1 - core], mate).wait_recv()
+        go(line(n, 1, DG.at[n, yy], 2 * y_one + core))
+        go(line(n, 2, DG.at[n, yy], 2 * y_two + core))
+
+    def line_on(n):
+        line(n, 1, DG.at[n, y_one], 2 * y_one + core).wait_recv()
+        go(line(n, 3, DG.at[n, y_one], 2 * y_two + core))
+
+    def line_end(n):
+        line(n, 2, DG.at[n, y_two], 2 * y_two + core).wait_recv()
+        line(n, 3, DG.at[n, y_last], 2 * y_two + core).wait_recv()
+
+    line_start(0)
+    line_send(0)
     for copy in edges:
         copy.wait_recv()
     for m in range(2):
         owned = (DKV[1, m] + wide(DKR[0, m]) + wide(DKR[1, m])).astype(BF16)
-        DKVS[m] = owned
         for h in range(2):
+            DQS[1 + h, m] = owned[:, 256 * h : 256 * h + 256]
             DQ[m, :, 384 * h + 128 : 384 * h + 384] = owned[:, 256 * h : 256 * h + 256]
-    line_start(DKVS, DGK, dk_s, dk_r)
+    line_start(1)
+    line_start(2)
     SB[2, 0] = dot(DQ[0], WQ[0], NT).astype(BF16)
     sum_start(2, 0)
-    line_send(DGK, dk_s, dk_r)
+    line_send(1)
+    line_send(2)
     SB[2, 1] = dot(DQ[1], WQ[1], NT).astype(BF16)
     sum_start(2, 1)
-    line_on(DGQ, dq_s, dq_r)
+    line_on(0)
+
+    c_one = c + 1 - 2 * lax.rem(c, 2)
+    c_two = lax.rem(c + 2, 4)
+    c_not = lax.rem(c_one + 2, 4)
+    mine = pl.ds(pl.multiple_of(64 * core, 64), 64)
+    theirs = pl.ds(pl.multiple_of(64 * (1 - core), 64), 64)
+
+    def clip_start(n):
+        for k, block in ((0, c_one), (1, c_not)):
+            go(remote(W.at[n, block], WR.at[n, k], cl_s.at[n, k], cl_r.at[n, k], {"clip": c_one}))
+
+    def clip_on(n):
+        for k, block in ((1, c_two), (0, c)):
+            part = WR.at[n, k]
+            remote(part, part, cl_s.at[n, k], cl_r.at[n, k], {"clip": c_one}).wait_recv()
+            WS[n, k] = (wide(W[n, block]) + wide(WR[n, k])).astype(BF16)
+            if k == 1:
+                for j, half, device in ((2, mine, {"clip": c_two}), (3, theirs, {"clip": c_two, "vid": mate})):
+                    go(remote(WS.at[n, 1, half], WF.at[n, core, 1], cl_s.at[n, j], wf_r.at[n, core, 1], device))
+            else:
+                go(remote(WS.at[n, 0, theirs], WF.at[n, core, 0], cl_s.at[n, 4], wf_r.at[n, core, 0], {"vid": mate}))
+                WF[n, core, 0] = WS[n, 0, mine, :]
+
+    def clip_end(n):
+        for src, k, device in (
+            (core, 1, {"clip": c_two}), (1 - core, 1, {"clip": c_two, "vid": mate}), (1 - core, 0, {"vid": mate})
+        ):
+            part = WF.at[n, src, k]
+            remote(part, part, cl_s.at[n, 2], wf_r.at[n, src, k], device).wait_recv()
+        return [wide(WF[n, m, 0]) + wide(WF[n, m, 1]) for m in range(2)]
+
+    def line_grad(n):
+        line_end(n)
+        W[n] = dot(NGT[...], DG[n].reshape(1024, 256), NN).astype(BF16).reshape(4, 128, 256)
+        clip_start(n)
+
+    sum_1(2)
+    line_on(1)
+    line_grad(0)
+    sum_2(2)
+    line_on(2)
+    line_grad(1)
     spread(lambda k, y: GS.at[k, :, y], GG, gg_s, gg_r, distant)
-
-    def clip_start(send, got, s_sem, r_sem):
-        for d in range(4):
-            peer = lax.rem(c + d, 4)
-            for k in range(2):
-                to = lax.rem(core + 1 - k, 2)
-                half = pl.ds(pl.multiple_of(64 * to, 64), 64)
-                if d == 0 and k == 1:
-                    got[core, c] = send[c, half, :]
-                else:
-                    device = {"clip": peer, "vid": 2 * yy + to}
-                    go(remote(send.at[peer, half], got.at[core, c], s_sem.at[to, peer], r_sem.at[core, c], device))
-
-    def clip_end(got, s_sem, r_sem):
-        for d in range(4):
-            peer = lax.rem(c + d, 4)
-            for k in range(2):
-                if d == 0 and k == 1:
-                    continue
-                to = lax.rem(core + 1 - k, 2)
-                part = got.at[to, peer]
-                device = {"clip": peer, "vid": 2 * yy + to}
-                remote(part, part, s_sem.at[to, peer], r_sem.at[to, peer], device).wait_recv()
-
-    def clip_sum(got, m):
-        return (wide(got[m, 0]) + wide(got[m, 1])) + (wide(got[m, 2]) + wide(got[m, 3]))
-
-    sum_1(2)
-    line_on(DGK, dk_s, dk_r)
-    line_end(DGQ, dq_s, dq_r)
-    dq_all = DGQ[...].reshape(1024, 256)
-    WA[...] = dot(NGT[...], dq_all, NN).astype(BF16).reshape(4, 128, 256)
-    clip_start(WA, RA, wa_s, wa_r)
-    sum_2(2)
-    line_end(DGK, dk_s, dk_r)
-    dk_all = DGK[...].reshape(1024, 512)
-    WB[...] = dot(NGT[...], dk_all, NN).astype(BF16).reshape(4, 128, 512)
-    clip_start(WB, RB, wb_s, wb_r)
+    clip_on(0)
+    line_grad(2)
     for g, m in chunks:
         cur = wide(xs[m][own[g, m], :])
         inv = lax.rsqrt(jnp.mean(cur * cur, -1, keepdims=True) + EPSILON)
         scaled = summed(2, g, m) * MODS[2 + m : 3 + m, :]
         back = inv * scaled - cur * (inv * inv * inv) * jnp.mean(scaled * cur, -1, keepdims=True)
         share(2, g, m, DIFF[g, m] + back)
+    clip_on(1)
     collect(GG, gg_s, gg_r)
     o_all = OG[...].reshape(1024, 256)
     for s in range(4):
-        WC[s] = dot(GG[:, s].reshape(1024, 128), o_all, TN).astype(BF16)
-    clip_start(WC, RC, wc_s, wc_r)
+        W[3, s] = dot(GG[:, s].reshape(1024, 128), o_all, TN).astype(BF16)
+    clip_start(3)
     share_on(2)
+    clip_on(2)
+    clip_on(3)
     q_outs = (qv_out, qa_out)
     o_outs = (ov_out, oa_out)
-    clip_end(RA, wa_s, wa_r)
-    for m in range(2):
-        total = clip_sum(RA, m)
+    for m, total in enumerate(clip_end(0)):
         for h in range(2):
             q_outs[m][:, h, 0:128] = total[:, 128 * h : 128 * h + 128]
-    share_end(2)
-    outs = (
-        pltpu.make_async_copy(AG.at[2, 0], dv_out, o_sem.at[0]),
-        pltpu.make_async_copy(AG.at[2, 1], da_out, o_sem.at[1]),
-    )
-    for copy in outs:
-        copy.start()
-    clip_end(RB, wb_s, wb_r)
-    for m in range(2):
-        total = clip_sum(RB, m)
-        for h in range(2):
-            q_outs[m][:, h, 128:384] = total[:, 256 * h : 256 * h + 256]
-    clip_end(RC, wc_s, wc_r)
-    for m in range(2):
-        total = clip_sum(RC, m)
+    for h in range(2):
+        if h == 1:
+            share_end(2)
+            outs = (
+                pltpu.make_async_copy(AG.at[2, 0], dv_out, o_sem.at[0]),
+                pltpu.make_async_copy(AG.at[2, 1], da_out, o_sem.at[1]),
+            )
+            for copy in outs:
+                copy.start()
+        for m, total in enumerate(clip_end(1 + h)):
+            q_outs[m][:, h, 128:384] = total
+    for m, total in enumerate(clip_end(3)):
         for h in range(2):
             o_outs[m][h] = total[:, 128 * h : 128 * h + 128]
     for copy in outs:
@@ -505,19 +510,18 @@
         scratch_shapes=[
             vm((2, 2048, 768)), vm((2, 256, 2048)), vm((2, 2, 128, 2048)), vm((2, 4, 4, 128, 128)),
             vm((8, 4, 128, 128)), vm((512, 1024)), vm((3, 2, 128, 256)), vm((8, 128, 256)),
-            vm((2, 4, 4, 128, 128)), vm((8, 4, 128, 128)), vm((2, 128, 768)), vm((2, 128, 256)),
-            vm((2, 128, 512)), vm((4, 2, 128, 256)), vm((4, 2, 128, 512)), vm((3, 2, 128, 256)),
+            vm((2, 4, 4, 128, 128)), vm((8, 4, 128, 128)), vm((2, 128, 768)), vm((3, 2, 128, 256)),
+            vm((3, 4, 2, 128, 256)), vm((3, 2, 128, 256)),
             vm((3, 3, 2, 128, 512)), vm((4, 128, 768), F32), vm((2, 128, 2048), F32),
             vm((3, 2, 128, 2048)), vm((3, 2, 2, 2, 16, 2048)), vm((3, 2, 2, 16, 2048)),
             vm((3, 2, 2, 16, 2048)), vm((3, 2, 2, 16, 2048)), vm((3, 2, 2, 16, 2048)),
             vm((3, 2, 128, 2048)), vm((2, 2, 16, 2048), F32), vm((2, 128, 256)),
             vm((3, 2, 128, 512), F32), vm((2, 2, 128, 512)), vm((2, 2, 128, 512)),
-            vm((4, 128, 256)), vm((2, 4, 64, 256)), vm((4, 128, 512)), vm((2, 4, 64, 512)),
-            vm((4, 128, 256)), vm((2, 4, 64, 256)), vm((8, 2048), F32), vm((2, 128, 768), F32),
+            vm((4, 4, 128, 256)), vm((4, 2, 128, 256)), vm((4, 2, 128, 256)), vm((4, 2, 2, 64, 256)),
+            vm((8, 2048), F32), vm((2, 128, 768), F32),
             dma((4,)), dma((2,)), dma((8,)), dma((8,)), dma((3, 2, 2, 7)), dma((3, 2, 2, 7)),
             dma((8,)), dma((8,)), dma((8,)), dma((8,)), dma((8,)), dma((8,)),
-            dma((4,)), dma((4,)), dma((4,)), dma((4,)),
-            dma((2, 4)), dma((2, 4)), dma((2, 4)), dma((2, 4)), dma((2, 4)), dma((2, 4)),
+            dma((3, 4)), dma((3, 4)), dma((4, 5)), dma((4, 2)), dma((4, 2, 2)),
         ],
         compiler_params=pltpu.CompilerParams(
             collective_id=0, has_side_effects=True, vmem_limit_bytes=VMEM_LIMIT
@@ -526,16 +530,33 @@
     )(*operands)
 
 
+def finish_kernel(*refs):
+    for src, dst in zip(refs[:6], refs[6:]):
+        dst[...] = src[...]
+
+
+def finish(*results):
+    inside = pl.BlockSpec(memory_space=pltpu.VMEM)
+    return pl.pallas_call(
+        finish_kernel,
+        out_shape=tuple(jax.ShapeDtypeStruct(r.shape, r.dtype) for r in results),
+        in_specs=[inside] * 6,
+        out_specs=(inside,) * 6,
+        compiler_params=pltpu.CompilerParams(vmem_limit_bytes=8 * 1024 * 1024),
+        name="finish",
+    )(*results)
+
+
 def local(
     video_tokens, audio_tokens, qkv_video, out_video, qkv_audio, out_audio, gain_video, gain_audio,
     time_from, time_to, time_steps, windows, intersection,
 ):
-    d_video, d_audio, qv, qa, ov, oa = fused(
-        time_steps, windows, intersection, video_tokens[0], audio_tokens[0],
+    d_video, d_audio, qv, qa, ov, oa = finish(*fused(
+        time_steps, windows, intersection.swapaxes(1, 2), video_tokens[0], audio_tokens[0],
         gain_video.reshape(1, 2048), gain_audio.reshape(1, 2048), time_from, time_to,
         qkv_video.reshape(2048, 768), qkv_audio.reshape(2048, 768),
         out_video.reshape(256, 2048), out_audio.reshape(256, 2048),
-    )
+    ))
     return d_video[None], d_audio[None], qv, ov.swapaxes(1, 2), qa, oa.swapaxes(1, 2)
 
 

time: 167 us -> 159 us (0.952)
  the two profiles are of different devices: /device:TPU:232 before, /device:TPU:1 now
where the time goes in v3:
time: 159 us; the launch traced here: 156 us
  Pallas kernels  143 us (90%)
  local copies, waits for them, and re-layouts  12.3 us (8%)
    pallas_call x1, Pallas kernels, fused(): pl.pallas_call(kernel, out_shape=(shape((128, 2048), BF16), shape((128, 2...  141 us
    unnamed x16, local copies, waits for them, and re-layouts  12.3 us

profile of v3, /device:TPU:1, one launch (start us, length us, event | category | flops | bytes accessed | tf_op | source)
XLA Modules:
  0.0 155.6 jit_solution(4809445488436896279)
XLA Ops:
  0.6 0.0 copy-start.6
  0.6 4.3 %copy.19 = bf16[256,8,2,384]{3,1,2,0:T(8,128)(2,1)} copy(bf16[256,8,2,384]{3,2,1,0:T(2,128)(2,1)} %bitcast.17) | data formatting | bytes 6291456
  5.0 0.0 copy-done.6
  5.0 2.3 %copy.20 = bf16[256,8,2,384]{3,1,2,0:T(8,128)(2,1)} copy(bf16[256,8,2,384]{3,2,1,0:T(2,128)(2,1)S(1)} %bitcast.18) | data formatting | bytes 6291456
  7.3 141.4 %step.1 = (bf16[128,2048]{1,0:T(8,128)(2,1)}, bf16[128,2048]{1,0:T(8,128)(2,1)}, f32[64,2,384]{2,1,0:T(2,128)}, f32[64,2,384]{2,1,0:T(2,128)}, f32[2,64,128]{2,1,0:T(8,128)}, /*index=5*/f32[2,64,128]{2,1,0:T(8,128)}) custom-call(s32[1,2]{1,0:T(1,128)} %steps.1, s32[1,2]{1,0:T(1,128)} %windows.1, s32[1,2,32]{2,1,0:T(2,128)} %bitcast.25, ...), custom_call_target="tpu_custom_call" | custom-call | tf_op jit(solution)/shard_map/step/pallas_call | solution.py:502
  148.7 0.0 copy-start
  148.7 1.0 copy-done
  149.7 0.0 copy-start.1
  149.7 1.0 copy-done.1
  150.8 0.0 copy-start.2
  150.8 0.9 copy-done.2
  151.7 0.0 copy-start.3
  151.7 0.9 copy-done.3
  152.6 0.0 copy-start.4
  152.6 0.8 copy-done.4
  153.5 0.0 copy-start.5
  153.5 0.8 copy-done.5
  154.3 1.2 finish.1
Async XLA Ops:
  0.6 4.3 %copy-start.6 = (bf16[2048,2,384]{2,1,0:T(2,128)(2,1)S(1)}, bf16[2048,2,384]{2,1,0:T(2,128)(2,1)}, u32[]{:S(2)}) copy-start(bf16[2048,2,384]{2,1,0:T(2,128)(2,1)} %param.17) | copy-start | bytes 9437188
  148.7 1.0 copy-start
  149.7 1.0 copy-start.1
  150.8 0.9 copy-start.2
  151.7 0.9 copy-start.3
  152.6 0.8 copy-start.4
  153.5 0.8 copy-start.5

commit v4 on v3

--- a/solution.py
+++ b/solution.py
@@ -16,7 +16,7 @@
 TN = (((0,), (0,)), ((), ()))
 NN = (((1,), (0,)), ((), ()))
 T1, ST, T2 = 0, 1, 2
-VMEM_LIMIT = 62 * 1024 * 1024
+VMEM_LIMIT = 42 * 1024 * 1024
 
 
 def dot(a, b, dims):
@@ -26,10 +26,10 @@
 def kernel(
     steps, windows, ranges, xv, xa, gv, ga, tf, tt, wqv, wqa, wov, woa,
     dv_out, da_out, qv_out, qa_out, ov_out, oa_out,
-    WQ, WO, N0, NS, NG, NGT, OB, OG, GS, GG, DQ, DQS, DG, QR, KV, PS, ACC,
+    N0, NS, NG, NGT, OB, OG, GS, GG, DQ, DQS, DG, QR, KV, PS, ACC,
     SB, R1, S2, R2, ZS, ZR, AG, DIFF, DO, DKV, DKS, DKR,
     W, WR, WS, WF, MODS, BIAS,
-    w_sem, o_sem, kv_s, kv_r, ar_s, ar_r, ng_s, ng_r, og_s, og_r, gg_s, gg_r,
+    kv_s, kv_r, ar_s, ar_r, ng_s, ng_r, og_s, og_r, gg_s, gg_r,
     dg_s, dg_r, cl_s, cl_r, wf_r,
 ):
     v = lax.axis_index("vid")
@@ -72,15 +72,6 @@
         give[g, m] = rows(away + 16 * (1 - keepf[m]))
         hold[g, m] = rows(away + 16 * keepf[m])
 
-    loads = [
-        pltpu.make_async_copy(wqv, WQ.at[0], w_sem.at[0]),
-        pltpu.make_async_copy(wqa, WQ.at[1], w_sem.at[1]),
-        pltpu.make_async_copy(wov, WO.at[0], w_sem.at[2]),
-        pltpu.make_async_copy(woa, WO.at[1], w_sem.at[3]),
-    ]
-    for load in loads:
-        load.start()
-
     barrier = pltpu.get_barrier_semaphore()
     greet = [{"vid": lax.rem(v + d, 8)} for d in range(1, 8)]
     greet += [{"aud": peer} for peer in (near, far, across)]
@@ -89,6 +80,8 @@
     for peer in greet:
         pl.semaphore_signal(barrier, 1, device_id=peer, device_id_type=MESH)
 
+    WQ = (wqv, wqa)
+    WO = (wov, woa)
     pending = []
 
     def remote(src, dst, send, recv, device):
@@ -154,8 +147,7 @@
 
         lax.fori_loop(0, 4, norm_teacher, 0)
     for m in range(2):
-        loads[m].wait()
-        store_qkv(T1, m, dot(N0[T1, m], WQ[m], NN))
+        store_qkv(T1, m, dot(N0[T1, m], WQ[m][...], NN))
     pl.semaphore_wait(barrier, len(greet))
     kv_start(T1)
 
@@ -168,7 +160,7 @@
             return carry
 
         lax.fori_loop(0, 4, norm_student, 0)
-        store_qkv(ST, m, dot(N0[ST, m], WQ[m], NN))
+        store_qkv(ST, m, dot(N0[ST, m], WQ[m][...], NN))
     kv_start(ST)
 
     qpos = lax.broadcasted_iota(jnp.int32, (128, 128), 0)
@@ -231,7 +223,7 @@
             OB[net, m, :, 128 * h : 128 * h + 128] = dot(prob.astype(BF16), values, NN).astype(BF16)
 
     def project_out(net, m):
-        return dot(OB[net, m], WO[m], NN)
+        return dot(OB[net, m], WO[m][...], NN)
 
     def aud(i, g, m, kind, src, dst, device):
         return remote(src, dst, ar_s.at[i, g, m, kind], ar_r.at[i, g, m, kind], {"aud": device})
@@ -279,8 +271,6 @@
             part = AG.at[i, m, give[g, m]]
             aud(i, g, m, 6, part, part, first[m]).wait_recv()
 
-    for m in range(2):
-        loads[2 + m].wait()
     kv_wait(T1)
     for m in range(2):
         attention(T1, m, False)
@@ -307,7 +297,7 @@
     share_end(0)
 
     for m in range(2):
-        store_qkv(T2, m, dot(AG[0, m], WQ[m], NN))
+        store_qkv(T2, m, dot(AG[0, m], WQ[m][...], NN))
     kv_start(T2)
     kv_wait(T2)
     for m in range(2):
@@ -333,7 +323,7 @@
     GG[v] = GS[core, :, yy]
     spread(lambda k, y: GS.at[k, :, y], GG, gg_s, gg_r, close)
     for m in range(2):
-        DO[m] = dot(AG[1, m], WO[m], NT).astype(BF16)
+        DO[m] = dot(AG[1, m], WO[m][...], NT).astype(BF16)
     for m in range(2):
         for h in range(2):
             cols = slice(256 * h, 256 * h + 128)
@@ -397,11 +387,11 @@
             DQ[m, :, 384 * h + 128 : 384 * h + 384] = owned[:, 256 * h : 256 * h + 256]
     line_start(1)
     line_start(2)
-    SB[2, 0] = dot(DQ[0], WQ[0], NT).astype(BF16)
+    SB[2, 0] = dot(DQ[0], WQ[0][...], NT).astype(BF16)
     sum_start(2, 0)
     line_send(1)
     line_send(2)
-    SB[2, 1] = dot(DQ[1], WQ[1], NT).astype(BF16)
+    SB[2, 1] = dot(DQ[1], WQ[1][...], NT).astype(BF16)
     sum_start(2, 1)
     line_on(0)
 
@@ -472,19 +462,13 @@
     for h in range(2):
         if h == 1:
             share_end(2)
-            outs = (
-                pltpu.make_async_copy(AG.at[2, 0], dv_out, o_sem.at[0]),
-                pltpu.make_async_copy(AG.at[2, 1], da_out, o_sem.at[1]),
-            )
-            for copy in outs:
-                copy.start()
+            dv_out[...] = AG[2, 0]
+            da_out[...] = AG[2, 1]
         for m, total in enumerate(clip_end(1 + h)):
             q_outs[m][:, h, 128:384] = total
     for m, total in enumerate(clip_end(3)):
         for h in range(2):
             o_outs[m][h] = total[:, 128 * h : 128 * h + 128]
-    for copy in outs:
-        copy.wait()
     for copy in pending:
         copy.wait_send()
 
@@ -497,7 +481,6 @@
     dma = pltpu.SemaphoreType.DMA
     inside = pl.BlockSpec(memory_space=pltpu.VMEM)
     scalar = pl.BlockSpec(memory_space=pltpu.SMEM)
-    outside = pl.BlockSpec(memory_space=pl.ANY)
     shape = jax.ShapeDtypeStruct
     return pl.pallas_call(
         kernel,
@@ -505,10 +488,10 @@
             shape((128, 2048), BF16), shape((128, 2048), BF16), shape((64, 2, 384), F32),
             shape((64, 2, 384), F32), shape((2, 64, 128), F32), shape((2, 64, 128), F32),
         ),
-        in_specs=[scalar] * 3 + [inside] * 6 + [outside] * 4,
-        out_specs=(outside, outside, inside, inside, inside, inside),
+        in_specs=[scalar] * 3 + [inside] * 10,
+        out_specs=(inside,) * 6,
         scratch_shapes=[
-            vm((2, 2048, 768)), vm((2, 256, 2048)), vm((2, 2, 128, 2048)), vm((2, 4, 4, 128, 128)),
+            vm((2, 2, 128, 2048)), vm((2, 4, 4, 128, 128)),
             vm((8, 4, 128, 128)), vm((512, 1024)), vm((3, 2, 128, 256)), vm((8, 128, 256)),
             vm((2, 4, 4, 128, 128)), vm((8, 4, 128, 128)), vm((2, 128, 768)), vm((3, 2, 128, 256)),
             vm((3, 4, 2, 128, 256)), vm((3, 2, 128, 256)),
@@ -519,7 +502,7 @@
             vm((3, 2, 128, 512), F32), vm((2, 2, 128, 512)), vm((2, 2, 128, 512)),
             vm((4, 4, 128, 256)), vm((4, 2, 128, 256)), vm((4, 2, 128, 256)), vm((4, 2, 2, 64, 256)),
             vm((8, 2048), F32), vm((2, 128, 768), F32),
-            dma((4,)), dma((2,)), dma((8,)), dma((8,)), dma((3, 2, 2, 7)), dma((3, 2, 2, 7)),
+            dma((8,)), dma((8,)), dma((3, 2, 2, 7)), dma((3, 2, 2, 7)),
             dma((8,)), dma((8,)), dma((8,)), dma((8,)), dma((8,)), dma((8,)),
             dma((3, 4)), dma((3, 4)), dma((4, 5)), dma((4, 2)), dma((4, 2, 2)),
         ],
@@ -531,18 +514,24 @@
 
 
 def finish_kernel(*refs):
-    for src, dst in zip(refs[:6], refs[6:]):
-        dst[...] = src[...]
+    sources, targets, sems = refs[:6], refs[6:12], refs[12]
+    leave = [pltpu.make_async_copy(x, y, sems.at[i]) for i, (x, y) in enumerate(zip(sources, targets))]
+    for copy in leave:
+        copy.start()
+    for copy in leave:
+        copy.wait()
 
 
 def finish(*results):
     inside = pl.BlockSpec(memory_space=pltpu.VMEM)
+    outside = pl.BlockSpec(memory_space=pl.ANY)
     return pl.pallas_call(
         finish_kernel,
         out_shape=tuple(jax.ShapeDtypeStruct(r.shape, r.dtype) for r in results),
         in_specs=[inside] * 6,
-        out_specs=(inside,) * 6,
-        compiler_params=pltpu.CompilerParams(vmem_limit_bytes=8 * 1024 * 1024),
+        out_specs=(outside,) * 6,
+        scratch_shapes=[pltpu.SemaphoreType.DMA((6,))],
+        compiler_params=pltpu.CompilerParams(vmem_limit_bytes=4 * 1024 * 1024),
         name="finish",
     )(*results)
 

time: 159 us -> 150 us (0.943); the launches traced: 156 us -> 149 us
  local copies, waits for them, and re-layouts: 12.3 us -> 4.95 us
    unnamed x16 -> x26, local copies, waits for them, and re-layouts: 12.3 us -> 4.95 us
where the time goes in v4:
time: 150 us; the launch traced here: 149 us
  Pallas kernels  143 us (95%)
  local copies, waits for them, and re-layouts  4.95 us (3%)
    pallas_call x1, Pallas kernels, fused(): pl.pallas_call(kernel, out_shape=(shape((128, 2048), BF16), shape((128, 2...  142 us
    unnamed x26, local copies, waits for them, and re-layouts  4.95 us

profile of v4, /device:TPU:1, one launch (start us, length us, event | category | flops | bytes accessed | tf_op | source)
XLA Modules:
  0.0 148.9 jit_solution(11945580083454887077)
XLA Ops:
  0.6 0.0 copy-start.11
  0.6 2.7 %copy.19 = bf16[256,8,2,384]{3,1,2,0:T(8,128)(2,1)S(1)} copy(bf16[256,8,2,384]{3,2,1,0:T(2,128)(2,1)} %bitcast.24) | data formatting | bytes 6291456
  3.3 0.1 copy-done.11
  3.5 0.0 copy-start
  3.5 0.0 copy-start.1
  3.5 0.0 copy-start.2
  3.5 0.0 copy-start.3
  3.5 0.0 copy-start.4
  3.5 0.0 copy-start.5
  3.5 0.0 copy-start.6
  3.5 0.0 copy-start.7
  3.5 0.0 copy-start.8
  3.5 0.0 copy-start.9
  3.6 0.0 copy-start.10
  3.6 0.6 copy.20
  4.2 0.5 copy-done
  4.7 0.3 copy-done.1
  5.0 0.2 copy-done.2
  5.2 0.2 copy-done.3
  5.4 0.2 copy-done.4
  5.5 0.1 copy-done.5
  5.7 0.0 copy-done.6
  5.7 0.0 copy-done.7
  5.7 0.0 copy-done.8
  5.7 0.0 copy-done.9
  5.7 0.0 copy-done.10
  5.7 141.8 %step.1 = (bf16[128,2048]{1,0:T(8,128)(2,1)S(1)}, bf16[128,2048]{1,0:T(8,128)(2,1)S(1)}, f32[64,2,384]{2,1,0:T(2,128)S(1)}, f32[64,2,384]{2,1,0:T(2,128)S(1)}, f...) custom-call(s32[1,2]{1,0:T(1,128)S(1)} %copy-done.9, s32[1,2]{1,0:T(1,128)S(1)} %copy-done.10, ...), custom_call_target="tpu_custom_call" | custom-call | tf_op jit(solution)/shard_map/step/pallas_call | solution.py:485
  147.5 1.2 finish.1
Async XLA Ops:
  0.6 2.8 %copy-start.11 = (bf16[2048,2,384]{2,1,0:T(2,128)(2,1)S(1)}, bf16[2048,2,384]{2,1,0:T(2,128)(2,1)}, u32[]{:S(2)}) copy-start(bf16[2048,2,384]{2,1,0:T(2,128)(2,1)} %param.17) | copy-start | bytes 9437188
  3.5 1.2 copy-start
  3.5 1.5 %copy-start.1 = (bf16[2,128,2048]{2,1,0:T(8,128)(2,1)S(1)}, bf16[2,128,2048]{2,1,0:T(8,128)(2,1)}, u32[]{:S(2)}) copy-start(bf16[2,128,2048]{2,1,0:T(8,128)(2,1)} %param.18) | copy-start | bytes 3145732
  3.5 1.7 %copy-start.2 = (f32[65,2048]{1,0:T(8,128)S(1)}, f32[65,2048]{1,0:T(8,128)}, u32[]{:S(2)}) copy-start(f32[65,2048]{1,0:T(8,128)} %tf.1) | copy-start | bytes 1597444
  3.5 1.9 %copy-start.3 = (f32[65,2048]{1,0:T(8,128)S(1)}, f32[65,2048]{1,0:T(8,128)}, u32[]{:S(2)}) copy-start(f32[65,2048]{1,0:T(8,128)} %tt.1) | copy-start | bytes 1597444
  3.5 2.1 %copy-start.4 = (bf16[1,128,2048]{2,1,0:T(8,128)(2,1)S(1)}, bf16[1,128,2048]{2,1,0:T(8,128)(2,1)}, u32[]{:S(2)}) copy-start(bf16[1,128,2048]{2,1,0:T(8,128)(2,1)} %param.13) | copy-start | bytes 1572868
  3.5 2.2 %copy-start.5 = (bf16[1,128,2048]{2,1,0:T(8,128)(2,1)S(1)}, bf16[1,128,2048]{2,1,0:T(8,128)(2,1)}, u32[]{:S(2)}) copy-start(bf16[1,128,2048]{2,1,0:T(8,128)(2,1)} %param.14) | copy-start | bytes 1572868
  3.5 2.2 %copy-start.6 = (f32[2048]{0:T(1024)S(1)}, f32[2048]{0:T(1024)}, u32[]{:S(2)}) copy-start(f32[2048]{0:T(1024)} %param.19) | copy-start | bytes 24580
  3.5 2.1 %copy-start.7 = (f32[2048]{0:T(1024)S(1)}, f32[2048]{0:T(1024)}, u32[]{:S(2)}) copy-start(f32[2048]{0:T(1024)} %param.20) | copy-start | bytes 24580
  3.5 2.1 %copy-start.8 = (s32[1,32,2]{1,2,0:T(2,128)S(1)}, s32[1,32,2]{1,2,0:T(2,128)}, u32[]{:S(2)}) copy-start(s32[1,32,2]{1,2,0:T(2,128)} %param.25) | copy-start | bytes 772
  3.5 2.1 %copy-start.9 = (s32[1,2]{1,0:T(1,128)S(1)}, s32[1,2]{1,0:T(1,128)}, u32[]{:S(2)}) copy-start(s32[1,2]{1,0:T(1,128)} %steps.1) | copy-start | bytes 28
  3.6 2.1 %copy-start.10 = (s32[1,2]{1,0:T(1,128)S(1)}, s32[1,2]{1,0:T(1,128)}, u32[]{:S(2)}) copy-start(s32[1,2]{1,0:T(1,128)} %windows.1) | copy-start | bytes 28

commit v5 on v4

v5 whole, which is shorter than its diff:
```python
import jax
import jax.numpy as jnp
from jax import lax
from jax.experimental import pallas as pl
from jax.experimental.pallas import tpu as pltpu
from jax.sharding import PartitionSpec as P

BLK = 32
TGRID = 64
STEPS = 2
EPSILON = 1e-06
MESH = pl.DeviceIdType.MESH
F32 = jnp.float32
BF16 = jnp.bfloat16
NT = (((1,), (1,)), ((), ()))
TN = (((0,), (0,)), ((), ()))
NN = (((1,), (0,)), ((), ()))
T1, ST, T2 = 0, 1, 2
GG_EARLY = []
GG_LATE = [(0, 1), (1, 0), (3, 0), (1, 1), (3, 1), (2, 0), (2, 1)]
GROUPS = 2
PIECE = 32 // GROUPS
VMEM_LIMIT = 42 * 1024 * 1024


def dot(a, b, dims):
    return lax.dot_general(a, b, dims, preferred_element_type=F32)


def kernel(
    steps, windows, ranges, xv, xa, gv, ga, tf, tt, wqv, wqa, wov, woa,
    dv_out, da_out, qv_out, qa_out, ov_out, oa_out,
    N0, NS, NG, NGT, OB, OG, GS, GG, DQ, DG, QR, KV, PS, ACC,
    SB, R1, ZS, ZR, AG, DIFF, DO, DKV, DKS, DKR,
    WA, WR, WS, WF, WC, VR, VS, VF, MODS, BIAS,
    kv_s, kv_r, ar_s, ar_r, ng_s, ng_r, og_s, og_r, gg_s, gg_r,
    ed_s, ed_r, dg_s, dg_r, cl_s, cl_r, wf_r,
):
    v = lax.axis_index("vid")
    a = lax.axis_index("aud")
    c = lax.axis_index("clip")
    core = lax.rem(v, 2)
    yy = v // 2
    x = a // 2
    zh = lax.rem(a, 2)
    across = a + 1 - 2 * zh
    hops = (1, 3, 2)
    right = lax.rem(v + 1, 8)
    left = lax.rem(v + 7, 8)
    y_near = yy + 1 - 2 * lax.rem(yy, 2)
    y_far = 3 - yy
    y_one = (1 - core) * y_near + core * y_far
    y_two = core * y_near + (1 - core) * y_far
    y_last = 6 - yy - y_one - y_two
    mate = v + 1 - 2 * core

    def ahead(d):
        return lax.rem(x + d, 4)

    def piece(g, owner):
        return pl.ds(pl.multiple_of(PIECE * (4 * g + owner), PIECE), PIECE)

    chunks = [(g, m) for g in range(GROUPS) for m in range(2)]

    barrier = pltpu.get_barrier_semaphore()
    greet = [{"vid": lax.rem(v + d, 8)} for d in range(1, 8)]
    greet += [{"aud": peer} for peer in [2 * ahead(d) + zh for d in hops] + [across]]
    greet += [{"clip": c + 1 - 2 * lax.rem(c, 2)}]
    greet += [{"clip": lax.rem(c + 2, 4), "vid": 2 * yy + k} for k in range(2)]
    for peer in greet:
        pl.semaphore_signal(barrier, 1, device_id=peer, device_id_type=MESH)

    WQ = (wqv, wqa)
    WO = (wov, woa)
    pending = []

    def remote(src, dst, send, recv, device):
        return pltpu.make_async_remote_copy(
            src_ref=src, dst_ref=dst, send_sem=send, recv_sem=recv, device_id=device, device_id_type=MESH
        )

    def go(copy):
        copy.start()
        pending.append(copy)

    def wide(ref):
        return ref.astype(F32)

    now = steps[0, 0]
    stride = steps[0, 1]
    step = -stride.astype(F32) / TGRID
    conds = (
        tf[pl.ds(now, 1), :] + tt[pl.ds(now, 1), :],
        tf[pl.ds(now, 1), :] + tt[pl.ds(now - STEPS * stride, 1), :],
        tf[pl.ds(now - stride, 1), :] + tt[pl.ds(now - stride, 1), :],
    )
    gains = (gv, ga)
    for net in range(3):
        for m in range(2):
            MODS[2 * net + m : 2 * net + m + 1, :] = gains[m][...] * (1.0 + conds[net])

    xs = (xv, xa)

    def normed(net, m, r):
        part = pl.ds(pl.multiple_of(r * 32, 32), 32)
        cur = wide(xs[m][part, :])
        inv = lax.rsqrt(jnp.mean(cur * cur, -1, keepdims=True) + EPSILON)
        out = (cur * inv * MODS[2 * net + m : 2 * net + m + 1, :]).astype(BF16)
        N0[net, m, part, :] = out
        return part, out

    def make_qkv(net, rows_of, h):
        for m in range(2):
            rounded = dot(rows_of(m), WQ[m][:, 384 * h : 384 * h + 384], NN).astype(BF16)
            QR[net, m, :, 128 * h : 128 * h + 128] = rounded[:, 0:128]
            KV[net, h, 1, m] = rounded[:, 128:384]

    def kv_copies(net, h):
        return [
            remote(KV.at[net, h, 1], KV.at[net, h, 2 * k], kv_s.at[net, h, k], kv_r.at[net, h, k], {"vid": device})
            for k, device in enumerate((right, left))
        ]

    def kv_start(net, h):
        for copy in kv_copies(net, h):
            go(copy)

    def kv_wait(net, h):
        for copy in kv_copies(net, h):
            copy.wait_recv()

    for m in range(2):

        def norm_teacher(r, carry, m=m):
            normed(T1, m, r)
            return carry

        lax.fori_loop(0, 4, norm_teacher, 0)
    make_qkv(T1, lambda m: N0[T1, m], 0)
    pl.semaphore_wait(barrier, len(greet))
    kv_start(T1, 0)
    make_qkv(T1, lambda m: N0[T1, m], 1)
    kv_start(T1, 1)

    for m in range(2):

        def norm_student(r, carry, m=m):
            part, student = normed(ST, m, r)
            for s in range(16):
                NS[m, s // 4, s % 4, part, :] = student[:, 128 * s : 128 * s + 128]
            return carry

        lax.fori_loop(0, 4, norm_student, 0)
    for h in range(2):
        make_qkv(ST, lambda m: N0[ST, m], h)
        kv_start(ST, h)

    qpos = lax.broadcasted_iota(jnp.int32, (128, 128), 0)
    kpos = lax.broadcasted_iota(jnp.int32, (128, 128), 1)
    qblk = lax.broadcasted_iota(jnp.int32, (128, 1), 0) // BLK
    kblk = lax.broadcasted_iota(jnp.int32, (1, 128), 1) // BLK

    def spans(which, first_block, block_of):
        out = jnp.zeros(block_of.shape, jnp.int32)
        for i in range(4):
            at = jnp.clip(first_block + i, 0, 31)
            out = jnp.where(block_of == i, ranges[0, which, at], out)
        return out

    low_q = spans(0, 4 * v, qblk)
    high_q = spans(1, 4 * v, qblk)
    for slot in range(3):
        shard = v + slot - 1
        at = kpos + 128 * shard
        inside = (at >= 0) & (at < 1024)
        apart = jnp.abs(qpos - (kpos + 128 * (slot - 1)))
        keys_at = kblk + 4 * shard
        low_k = spans(0, 4 * shard, kblk)
        high_k = spans(1, 4 * shard, kblk)
        query_at = qblk + 4 * v
        tests = (
            (apart < windows[0, 0], (keys_at >= low_q) & (keys_at < high_q)),
            ((query_at >= low_k) & (query_at < high_k), apart < windows[0, 1]),
        )
        for m in range(2):
            for k in range(2):
                cols = slice(256 * slot + 128 * k, 256 * slot + 128 * k + 128)
                BIAS[m, :, cols] = jnp.where(inside & tests[m][k], 0.0, -1e30)

    def spread(src, dst, send, recv, offsets):
        for d in offsets:
            peer = 2 * lax.rem(yy + d[0], 4) + lax.rem(core + d[1], 2)
            go(remote(src(lax.rem(peer, 2), peer // 2), dst.at[v], send.at[peer], recv.at[v], {"vid": peer}))

    def collect(dst, send, recv):
        for d in range(1, 8):
            peer = lax.rem(v + d, 8)
            remote(dst.at[peer], dst.at[peer], send.at[peer], recv.at[peer], {"vid": peer}).wait_recv()

    whole = GG_EARLY + GG_LATE

    factor = 128 ** (-0.5)

    def attention(net, m, h, save=False):
        queries = QR[net, m, :, 128 * h : 128 * h + 128]
        keys = KV[net, h, :, :, :, 0:128].reshape(768, 128)
        values = KV[net, h, :, :, :, 128:256].reshape(768, 128)
        scores = dot(queries, keys, NT) * factor + BIAS[m]
        shifted = jnp.exp(scores - jnp.max(scores, -1, keepdims=True))
        prob = shifted * (1.0 / jnp.sum(shifted, -1, keepdims=True))
        if save:
            PS[2 * m + h] = prob
        OB[net, m, :, 128 * h : 128 * h + 128] = dot(prob.astype(BF16), values, NN).astype(BF16)

    def project_out(net, m):
        return dot(OB[net, m], WO[m][...], NN)

    def over_x(i, g, m, d, src, dst, kind):
        return remote(src, dst, ar_s.at[i, g, m, kind + d], ar_r.at[i, g, m, kind + d], {"aud": 2 * ahead(d) + zh})

    def over_z(i, g, m):
        return remote(ZS.at[i, g, m], ZR.at[i, g, m], ar_s.at[i, g, m, 0], ar_r.at[i, g, m, 0], {"aud": across})

    def sum_start(i, m):
        for g in range(GROUPS):
            for d in hops:
                go(over_x(i, g, m, d, SB.at[i, m, piece(g, ahead(d))], R1.at[i, g, m, d - 1], 0))

    def sum_on(i):
        for g, m in chunks:
            total = wide(SB[i, m, piece(g, x), :])
            for d in hops:
                over_x(i, g, m, d, R1.at[i, g, m, d - 1], R1.at[i, g, m, d - 1], 0).wait_recv()
                total = total + wide(R1[i, g, m, d - 1])
            ZS[i, g, m] = total.astype(BF16)
            go(over_z(i, g, m))

    def summed(i, g, m):
        over_z(i, g, m).wait_recv()
        return wide(ZS[i, g, m]) + wide(ZR[i, g, m])

    def share(i, g, m, value):
        AG[i, m, piece(g, x), :] = value.astype(BF16)
        part = AG.at[i, m, piece(g, x)]
        for d in hops:
            go(over_x(i, g, m, d, part, part, 3))

    def share_end(i):
        for g, m in chunks:
            for d in hops:
                part = AG.at[i, m, piece(g, ahead(4 - d))]
                over_x(i, g, m, d, part, part, 3).wait_recv()

    kv_wait(T1, 0)
    for m in range(2):
        attention(T1, m, 0)
    kv_wait(T1, 1)
    for m in range(2):
        attention(T1, m, 1)
        field = project_out(T1, m)
        SB[0, m] = field.astype(BF16)
        sum_start(0, m)
        ACC[m] = -field
    for h in range(2):
        kv_wait(ST, h)
    NG[v] = NS[core, :, yy]
    spread(lambda k, y: NS.at[k, :, y], NG, ng_s, ng_r, whole)
    for m in range(2):
        for h in range(2):
            attention(ST, m, h, True)
    OG[v] = OB[ST, core]
    spread(lambda k, y: OB.at[ST, k], OG, og_s, og_r, whole)
    sum_on(0)
    for m in range(2):
        ACC[m] = ACC[m] + 2.0 * project_out(ST, m)
    for g, m in chunks:
        cur = wide(xs[m][piece(g, x), :]) + step * summed(0, g, m)
        inv = lax.rsqrt(jnp.mean(cur * cur, -1, keepdims=True) + EPSILON)
        share(0, g, m, cur * inv * MODS[4 + m : 5 + m, :])
    share_end(0)

    for h in range(2):
        make_qkv(T2, lambda m: AG[0, m], h)
        kv_start(T2, h)
    kv_wait(T2, 0)
    for m in range(2):
        attention(T2, m, 0)
    kv_wait(T2, 1)
    for m in range(2):
        attention(T2, m, 1)
        SB[1, m] = (ACC[m] - project_out(T2, m)).astype(BF16)
        sum_start(1, m)
    collect(NG, ng_s, ng_r)
    for s in range(4):
        NGT[128 * s : 128 * s + 128, :] = NG[:, s].reshape(1024, 128).T
    collect(OG, og_s, og_r)
    sum_on(1)
    for g, m in chunks:
        diff = step * summed(1, g, m)
        DIFF[g, m] = diff
        share(1, g, m, 2.0 * step * diff)
    share_end(1)

    for m in range(2):
        DO[m] = dot(AG[1, m], WO[m][...], NT).astype(BF16)
    for m in range(2):
        for s in range(16):
            GS[m, s // 4, s % 4] = AG[1, m, :, 128 * s : 128 * s + 128]
    GG[v] = GS[core, :, yy]
    spread(lambda k, y: GS.at[k, :, y], GG, gg_s, gg_r, GG_EARLY)

    def backward(h):
        for m in range(2):
            queries = QR[ST, m, :, 128 * h : 128 * h + 128]
            keys = KV[ST, h, :, :, :, 0:128].reshape(768, 128)
            values = KV[ST, h, :, :, :, 128:256].reshape(768, 128)
            grad_out = DO[m, :, 128 * h : 128 * h + 128]
            prob = PS[2 * m + h]
            grad_prob = dot(grad_out, values, NT)
            center = jnp.sum(prob * grad_prob, -1, keepdims=True)
            dscore = (prob * (grad_prob - center) * factor).astype(BF16)
            DQ[h, m, :, 0:128] = dot(dscore, keys, NN).astype(BF16)
            dkey = dot(dscore, queries, TN).reshape(3, 2, 128, 128)
            dvalue = dot(prob.astype(BF16), grad_out, TN).reshape(3, 2, 128, 128)
            if m == 0:
                DKV[h, :, :, :, 0:128] = dkey
                DKV[h, :, :, :, 128:256] = dvalue
            else:
                for slot in (0, 2):
                    DKS[h, slot // 2, :, :, 0:128] = (DKV[h, slot, :, :, 0:128] + dkey[slot]).astype(BF16)
                    DKS[h, slot // 2, :, :, 128:256] = (DKV[h, slot, :, :, 128:256] + dvalue[slot]).astype(BF16)
                DKV[h, 1, :, :, 0:128] = DKV[h, 1, :, :, 0:128] + dkey[1]
                DKV[h, 1, :, :, 128:256] = DKV[h, 1, :, :, 128:256] + dvalue[1]

    def edges(h):
        return [
            remote(DKS.at[h, k], DKR.at[h, k], ed_s.at[h, k], ed_r.at[h, k], {"vid": device})
            for k, device in enumerate((left, right))
        ]

    def finish_kv(h):
        for copy in edges(h):
            copy.wait_recv()
        for m in range(2):
            DQ[h, m, :, 128:384] = (DKV[h, 1, m] + wide(DKR[h, 0, m]) + wide(DKR[h, 1, m])).astype(BF16)

    def line(n, k, part, device):
        return remote(part, part, dg_s.at[n, k], dg_r.at[n, k], {"vid": device})

    def line_start(n):
        DG[n, yy, core] = DQ[n, core]
        go(remote(DQ.at[n, 1 - core], DG.at[n, yy, core], dg_s.at[n, 0], dg_r.at[n, 0], {"vid": mate}))

    def line_send(n):
        line(n, 0, DG.at[n, yy, 1 - core], mate).wait_recv()
        go(line(n, 1, DG.at[n, yy], 2 * y_one + core))
        go(line(n, 2, DG.at[n, yy], 2 * y_two + core))

    def line_on(n):
        line(n, 1, DG.at[n, y_one], 2 * y_one + core).wait_recv()
        go(line(n, 3, DG.at[n, y_one], 2 * y_two + core))

    def line_end(n):
        line(n, 2, DG.at[n, y_two], 2 * y_two + core).wait_recv()
        line(n, 3, DG.at[n, y_last], 2 * y_two + core).wait_recv()

    for h in range(2):
        backward(h)
        for copy in edges(h):
            go(copy)
    finish_kv(0)
    line_start(0)
    for m in range(2):
        ACC[m] = dot(DQ[0, m], WQ[m][:, 0:384], NT)
    line_send(0)
    finish_kv(1)
    line_start(1)
    for m in range(2):
        SB[2, m] = (ACC[m] + dot(DQ[1, m], WQ[m][:, 384:768], NT)).astype(BF16)
        sum_start(2, m)
        if m == 0:
            line_send(1)
    line_on(0)

    c_one = c + 1 - 2 * lax.rem(c, 2)
    c_two = lax.rem(c + 2, 4)
    c_not = lax.rem(c_one + 2, 4)
    mine = pl.ds(pl.multiple_of(64 * core, 64), 64)
    theirs = pl.ds(pl.multiple_of(64 * (1 - core), 64), 64)

    parts = ((WA.at[0], WR.at[0], WS.at[0], WF.at[0]), (WA.at[1], WR.at[1], WS.at[1], WF.at[1]), (WC, VR, VS, VF))

    def clip_start(n):
        full, got, out, last = parts[n]
        for k, block in ((1, c_not), (0, c_one)):
            go(remote(full.at[block], got.at[k], cl_s.at[n, k], cl_r.at[n, k], {"clip": c_one}))

    def clip_on(n):
        full, got, out, last = parts[n]
        for k, block in ((1, c_two), (0, c)):
            part = got.at[k]
            remote(part, part, cl_s.at[n, k], cl_r.at[n, k], {"clip": c_one}).wait_recv()
            out[k] = (wide(full[block]) + wide(got[k])).astype(BF16)
            if k == 1:
                for j, half, device in ((2, mine, {"clip": c_two}), (3, theirs, {"clip": c_two, "vid": mate})):
                    go(remote(out.at[1, half], last.at[core, 1], cl_s.at[n, j], wf_r.at[n, core, 1], device))
            else:
                go(remote(out.at[0, theirs], last.at[core, 0], cl_s.at[n, 4], wf_r.at[n, core, 0], {"vid": mate}))
                last[core, 0] = out[0, mine, :]

    def clip_end(n):
        last = parts[n][3]
        for src, k, device in (
            (core, 1, {"clip": c_two}), (1 - core, 1, {"clip": c_two, "vid": mate}), (1 - core, 0, {"vid": mate})
        ):
            part = last.at[src, k]
            remote(part, part, cl_s.at[n, 2], wf_r.at[n, src, k], device).wait_recv()
        return [wide(last[m, 0]) + wide(last[m, 1]) for m in range(2)]

    def line_grad(n):
        line_end(n)
        WA[n] = dot(NGT[...], DG[n].reshape(1024, 384), NN).astype(BF16).reshape(4, 128, 384)
        clip_start(n)

    line_on(1)
    spread(lambda k, y: GS.at[k, :, y], GG, gg_s, gg_r, GG_LATE)
    sum_on(2)
    line_grad(0)
    line_grad(1)
    clip_on(0)
    for g, m in chunks:
        cur = wide(xs[m][piece(g, x), :])
        inv = lax.rsqrt(jnp.mean(cur * cur, -1, keepdims=True) + EPSILON)
        scaled = summed(2, g, m) * MODS[2 + m : 3 + m, :]
        back = inv * scaled - cur * (inv * inv * inv) * jnp.mean(scaled * cur, -1, keepdims=True)
        share(2, g, m, DIFF[g, m] + back)
    collect(GG, gg_s, gg_r)
    o_all = OG[...].reshape(1024, 256)
    for s in range(4):
        WC[s] = dot(GG[:, s].reshape(1024, 128), o_all, TN).astype(BF16)
    clip_start(2)
    clip_on(1)
    clip_on(2)
    q_outs = (qv_out, qa_out)
    o_outs = (ov_out, oa_out)
    for h in range(2):
        for m, total in enumerate(clip_end(h)):
            q_outs[m][:, h, :] = total
    share_end(2)
    dv_out[...] = AG[2, 0]
    da_out[...] = AG[2, 1]
    for m, total in enumerate(clip_end(2)):
        for h in range(2):
            o_outs[m][h] = total[:, 128 * h : 128 * h + 128]
    for copy in pending:
        copy.wait_send()


def vm(shape, kind=BF16):
    return pltpu.VMEM(shape, kind)


def fused(*operands):
    dma = pltpu.SemaphoreType.DMA
    inside = pl.BlockSpec(memory_space=pltpu.VMEM)
    scalar = pl.BlockSpec(memory_space=pltpu.SMEM)
    shape = jax.ShapeDtypeStruct
    return pl.pallas_call(
        kernel,
        out_shape=(
            shape((128, 2048), BF16), shape((128, 2048), BF16), shape((64, 2, 384), F32),
            shape((64, 2, 384), F32), shape((2, 64, 128), F32), shape((2, 64, 128), F32),
        ),
        in_specs=[scalar] * 3 + [inside] * 10,
        out_specs=(inside,) * 6,
        scratch_shapes=[
            vm((2, 2, 128, 2048)), vm((2, 4, 4, 128, 128)),
            vm((8, 4, 128, 128)), vm((512, 1024)), vm((3, 2, 128, 256)), vm((8, 128, 256)),
            vm((2, 4, 4, 128, 128)), vm((8, 4, 128, 128)), vm((2, 2, 128, 384)),
            vm((2, 4, 2, 128, 384)), vm((3, 2, 128, 256)),
            vm((3, 2, 3, 2, 128, 256)), vm((4, 128, 768), F32), vm((2, 128, 2048), F32),
            vm((3, 2, 128, 2048)), vm((3, GROUPS, 2, 3, PIECE, 2048)),
            vm((3, GROUPS, 2, PIECE, 2048)), vm((3, GROUPS, 2, PIECE, 2048)),
            vm((3, 2, 128, 2048)), vm((GROUPS, 2, PIECE, 2048), F32), vm((2, 128, 256)),
            vm((2, 3, 2, 128, 256), F32), vm((2, 2, 2, 128, 256)), vm((2, 2, 2, 128, 256)),
            vm((2, 4, 128, 384)), vm((2, 2, 128, 384)), vm((2, 2, 128, 384)), vm((2, 2, 2, 64, 384)),
            vm((4, 128, 256)), vm((2, 128, 256)), vm((2, 128, 256)), vm((2, 2, 64, 256)),
            vm((8, 2048), F32), vm((2, 128, 768), F32),
            dma((3, 2, 2)), dma((3, 2, 2)), dma((3, GROUPS, 2, 7)), dma((3, GROUPS, 2, 7)),
            dma((8,)), dma((8,)), dma((8,)), dma((8,)), dma((8,)), dma((8,)),
            dma((2, 2)), dma((2, 2)), dma((2, 4)), dma((2, 4)), dma((3, 5)), dma((3, 2)), dma((3, 2, 2)),
        ],
        compiler_params=pltpu.CompilerParams(
            collective_id=0, has_side_effects=True, vmem_limit_bytes=VMEM_LIMIT
        ),
        name="step",
    )(*operands)


def finish_kernel(*refs):
    sources, targets, sems = refs[:6], refs[6:12], refs[12]
    leave = [pltpu.make_async_copy(x, y, sems.at[i]) for i, (x, y) in enumerate(zip(sources, targets))]
    for copy in leave:
        copy.start()
    for copy in leave:
        copy.wait()


def finish(*results):
    inside = pl.BlockSpec(memory_space=pltpu.VMEM)
    outside = pl.BlockSpec(memory_space=pl.ANY)
    return pl.pallas_call(
        finish_kernel,
        out_shape=tuple(jax.ShapeDtypeStruct(r.shape, r.dtype) for r in results),
        in_specs=[inside] * 6,
        out_specs=(outside,) * 6,
        scratch_shapes=[pltpu.SemaphoreType.DMA((6,))],
        compiler_params=pltpu.CompilerParams(vmem_limit_bytes=4 * 1024 * 1024),
        name="finish",
    )(*results)


def local(
    video_tokens, audio_tokens, qkv_video, out_video, qkv_audio, out_audio, gain_video, gain_audio,
    time_from, time_to, time_steps, windows, intersection,
):
    d_video, d_audio, qv, qa, ov, oa = finish(*fused(
        time_steps, windows, intersection.swapaxes(1, 2), video_tokens[0], audio_tokens[0],
        gain_video.reshape(1, 2048), gain_audio.reshape(1, 2048), time_from, time_to,
        qkv_video.reshape(2048, 768), qkv_audio.reshape(2048, 768),
        out_video.reshape(256, 2048), out_audio.reshape(256, 2048),
    ))
    return d_video[None], d_audio[None], qv, ov.swapaxes(1, 2), qa, oa.swapaxes(1, 2)


def solution(mesh):
    return jax.shard_map(
        local,
        mesh=mesh,
        in_specs=(
            P("clip", "vid", None), P("clip", "vid", None), P(None, "aud", None), P("aud", None, None),
            P(None, "aud", None), P("aud", None, None), P(), P(), P(), P(),
            P("clip", None), P("clip", None), P("clip", None, None),
        ),
        out_specs=(
            P("clip", "vid", None), P("clip", "vid", None), P(("clip", "vid"), "aud", None),
            P("aud", None, ("clip", "vid")), P(("clip", "vid"), "aud", None), P("aud", None, ("clip", "vid")),
        ),
        check_vma=False,
    )
```

time: 150 us -> 141 us (0.940)
  Pallas kernels: 143 us -> 135 us
    pallas_call x1, Pallas kernels: 142 us -> 134 us  [fused(): pl.pallas_call(kernel, out_shape=(shape((128, 2048), BF16), shape((128, 2...]
where the time goes in v5:
time: 141 us
  Pallas kernels  135 us (96%)
  local copies, waits for them, and re-layouts  4.95 us (4%)
    pallas_call x1, Pallas kernels, fused(): pl.pallas_call(kernel, out_shape=(shape((128, 2048), BF16), shape((128, 2...  134 us
    unnamed x26, local copies, waits for them, and re-layouts  4.95 us

profile of v5, /device:TPU:1, one launch (start us, length us, event | category | flops | bytes accessed | tf_op | source)
XLA Modules:
  0.0 140.9 jit_solution(6258472687073910960)
XLA Ops:
  0.6 0.0 copy-start.11
  0.6 2.7 %copy.19 = bf16[256,8,2,384]{3,1,2,0:T(8,128)(2,1)S(1)} copy(bf16[256,8,2,384]{3,2,1,0:T(2,128)(2,1)} %bitcast.24) | data formatting | bytes 6291456
  3.3 0.1 copy-done.11
  3.5 0.0 copy-start
  3.5 0.0 copy-start.1
  3.5 0.0 copy-start.2
  3.5 0.0 copy-start.3
  3.5 0.0 copy-start.4
  3.5 0.0 copy-start.5
  3.5 0.0 copy-start.6
  3.5 0.0 copy-start.7
  3.5 0.0 copy-start.8
  3.5 0.0 copy-start.9
  3.6 0.0 copy-start.10
  3.6 0.6 copy.20
  4.2 0.5 copy-done
  4.7 0.3 copy-done.1
  5.0 0.2 copy-done.2
  5.2 0.2 copy-done.3
  5.4 0.2 copy-done.4
  5.5 0.1 copy-done.5
  5.7 0.0 copy-done.6
  5.7 0.0 copy-done.7
  5.7 0.0 copy-done.8
  5.7 0.0 copy-done.9
  5.7 0.0 copy-done.10
  5.7 133.9 %step.1 = (bf16[128,2048]{1,0:T(8,128)(2,1)S(1)}, bf16[128,2048]{1,0:T(8,128)(2,1)S(1)}, f32[64,2,384]{2,1,0:T(2,128)S(1)}, f32[64,2,384]{2,1,0:T(2,128)S(1)}, f...) custom-call(s32[1,2]{1,0:T(1,128)S(1)} %copy-done.9, s32[1,2]{1,0:T(1,128)S(1)} %copy-done.10, ...), custom_call_target="tpu_custom_call" | custom-call | tf_op jit(solution)/shard_map/step/pallas_call | solution.py:468
  139.6 1.2 finish.1
Async XLA Ops:
  0.6 2.8 %copy-start.11 = (bf16[2048,2,384]{2,1,0:T(2,128)(2,1)S(1)}, bf16[2048,2,384]{2,1,0:T(2,128)(2,1)}, u32[]{:S(2)}) copy-start(bf16[2048,2,384]{2,1,0:T(2,128)(2,1)} %param.17) | copy-start | bytes 9437188
  3.5 1.2 copy-start
  3.5 1.5 %copy-start.1 = (bf16[2,128,2048]{2,1,0:T(8,128)(2,1)S(1)}, bf16[2,128,2048]{2,1,0:T(8,128)(2,1)}, u32[]{:S(2)}) copy-start(bf16[2,128,2048]{2,1,0:T(8,128)(2,1)} %param.18) | copy-start | bytes 3145732
  3.5 1.7 %copy-start.2 = (f32[65,2048]{1,0:T(8,128)S(1)}, f32[65,2048]{1,0:T(8,128)}, u32[]{:S(2)}) copy-start(f32[65,2048]{1,0:T(8,128)} %tf.1) | copy-start | bytes 1597444
  3.5 1.9 %copy-start.3 = (f32[65,2048]{1,0:T(8,128)S(1)}, f32[65,2048]{1,0:T(8,128)}, u32[]{:S(2)}) copy-start(f32[65,2048]{1,0:T(8,128)} %tt.1) | copy-start | bytes 1597444
  3.5 2.1 %copy-start.4 = (bf16[1,128,2048]{2,1,0:T(8,128)(2,1)S(1)}, bf16[1,128,2048]{2,1,0:T(8,128)(2,1)}, u32[]{:S(2)}) copy-start(bf16[1,128,2048]{2,1,0:T(8,128)(2,1)} %param.13) | copy-start | bytes 1572868
  3.5 2.2 %copy-start.5 = (bf16[1,128,2048]{2,1,0:T(8,128)(2,1)S(1)}, bf16[1,128,2048]{2,1,0:T(8,128)(2,1)}, u32[]{:S(2)}) copy-start(bf16[1,128,2048]{2,1,0:T(8,128)(2,1)} %param.14) | copy-start | bytes 1572868
  3.5 2.2 %copy-start.6 = (f32[2048]{0:T(1024)S(1)}, f32[2048]{0:T(1024)}, u32[]{:S(2)}) copy-start(f32[2048]{0:T(1024)} %param.19) | copy-start | bytes 24580
  3.5 2.1 %copy-start.7 = (f32[2048]{0:T(1024)S(1)}, f32[2048]{0:T(1024)}, u32[]{:S(2)}) copy-start(f32[2048]{0:T(1024)} %param.20) | copy-start | bytes 24580
  3.5 2.1 %copy-start.8 = (s32[1,32,2]{1,2,0:T(2,128)S(1)}, s32[1,32,2]{1,2,0:T(2,128)}, u32[]{:S(2)}) copy-start(s32[1,32,2]{1,2,0:T(2,128)} %param.25) | copy-start | bytes 772
  3.5 2.1 %copy-start.9 = (s32[1,2]{1,0:T(1,128)S(1)}, s32[1,2]{1,0:T(1,128)}, u32[]{:S(2)}) copy-start(s32[1,2]{1,0:T(1,128)} %steps.1) | copy-start | bytes 28
  3.6 2.1 %copy-start.10 = (s32[1,2]{1,0:T(1,128)S(1)}, s32[1,2]{1,0:T(1,128)}, u32[]{:S(2)}) copy-start(s32[1,2]{1,0:T(1,128)} %windows.1) | copy-start | bytes 28

commit v6 on v5

--- a/solution.py
+++ b/solution.py
@@ -16,8 +16,6 @@
 TN = (((0,), (0,)), ((), ()))
 NN = (((1,), (0,)), ((), ()))
 T1, ST, T2 = 0, 1, 2
-GG_EARLY = []
-GG_LATE = [(0, 1), (1, 0), (3, 0), (1, 1), (3, 1), (2, 0), (2, 1)]
 GROUPS = 2
 PIECE = 32 // GROUPS
 VMEM_LIMIT = 42 * 1024 * 1024
@@ -30,7 +28,7 @@
 def kernel(
     steps, windows, ranges, xv, xa, gv, ga, tf, tt, wqv, wqa, wov, woa,
     dv_out, da_out, qv_out, qa_out, ov_out, oa_out,
-    N0, NS, NG, NGT, OB, OG, GS, GG, DQ, DG, QR, KV, PS, ACC,
+    N0, NS, NG, NGT, OB, OG, GS, GG, DQ, DG, QR, KV, PS, PT, ACC,
     SB, R1, ZS, ZR, AG, DIFF, DO, DKV, DKS, DKR,
     WA, WR, WS, WF, WC, VR, VS, VF, MODS, BIAS,
     kv_s, kv_r, ar_s, ar_r, ng_s, ng_r, og_s, og_r, gg_s, gg_r,
@@ -60,7 +58,7 @@
     def piece(g, owner):
         return pl.ds(pl.multiple_of(PIECE * (4 * g + owner), PIECE), PIECE)
 
-    chunks = [(g, m) for g in range(GROUPS) for m in range(2)]
+    chunks = [(g, m) for m in range(2) for g in range(GROUPS)]
 
     barrier = pltpu.get_barrier_semaphore()
     greet = [{"vid": lax.rem(v + d, 8)} for d in range(1, 8)]
@@ -109,25 +107,26 @@
         N0[net, m, part, :] = out
         return part, out
 
-    def make_qkv(net, rows_of, h):
-        for m in range(2):
-            rounded = dot(rows_of(m), WQ[m][:, 384 * h : 384 * h + 384], NN).astype(BF16)
-            QR[net, m, :, 128 * h : 128 * h + 128] = rounded[:, 0:128]
-            KV[net, h, 1, m] = rounded[:, 128:384]
-
-    def kv_copies(net, h):
+    def make_qkv(net, rows, h, m):
+        rounded = dot(rows, WQ[m][:, 384 * h : 384 * h + 384], NN).astype(BF16)
+        QR[net, m, :, 128 * h : 128 * h + 128] = rounded[:, 0:128]
+        KV[net, h, 1, m] = rounded[:, 128:384]
+
+    def kv_copies(net, h, m):
+        sent = KV.at[net, h, 1, m]
         return [
-            remote(KV.at[net, h, 1], KV.at[net, h, 2 * k], kv_s.at[net, h, k], kv_r.at[net, h, k], {"vid": device})
+            remote(sent, KV.at[net, h, 2 * k, m], kv_s.at[net, h, m, k], kv_r.at[net, h, m, k], {"vid": device})
             for k, device in enumerate((right, left))
         ]
 
-    def kv_start(net, h):
-        for copy in kv_copies(net, h):
+    def kv_start(net, h, m):
+        for copy in kv_copies(net, h, m):
             go(copy)
 
     def kv_wait(net, h):
-        for copy in kv_copies(net, h):
-            copy.wait_recv()
+        for m in range(2):
+            for copy in kv_copies(net, h, m):
+                copy.wait_recv()
 
     for m in range(2):
 
@@ -136,11 +135,14 @@
             return carry
 
         lax.fori_loop(0, 4, norm_teacher, 0)
-    make_qkv(T1, lambda m: N0[T1, m], 0)
+    for m in range(2):
+        make_qkv(T1, N0[T1, m], 0, m)
     pl.semaphore_wait(barrier, len(greet))
-    kv_start(T1, 0)
-    make_qkv(T1, lambda m: N0[T1, m], 1)
-    kv_start(T1, 1)
+    for m in range(2):
+        kv_start(T1, 0, m)
+    for m in range(2):
+        make_qkv(T1, N0[T1, m], 1, m)
+        kv_start(T1, 1, m)
 
     for m in range(2):
 
@@ -152,8 +154,9 @@
 
         lax.fori_loop(0, 4, norm_student, 0)
     for h in range(2):
-        make_qkv(ST, lambda m: N0[ST, m], h)
-        kv_start(ST, h)
+        for m in range(2):
+            make_qkv(ST, N0[ST, m], h, m)
+            kv_start(ST, h, m)
 
     qpos = lax.broadcasted_iota(jnp.int32, (128, 128), 0)
     kpos = lax.broadcasted_iota(jnp.int32, (128, 128), 1)
@@ -197,7 +200,7 @@
             peer = lax.rem(v + d, 8)
             remote(dst.at[peer], dst.at[peer], send.at[peer], recv.at[peer], {"vid": peer}).wait_recv()
 
-    whole = GG_EARLY + GG_LATE
+    whole = [(0, 1), (1, 0), (3, 0), (1, 1), (3, 1), (2, 0), (2, 1)]
 
     factor = 128 ** (-0.5)
 
@@ -245,8 +248,8 @@
         for d in hops:
             go(over_x(i, g, m, d, part, part, 3))
 
-    def share_end(i):
-        for g, m in chunks:
+    def share_end(i, m):
+        for g in range(GROUPS):
             for d in hops:
                 part = AG.at[i, m, piece(g, ahead(4 - d))]
                 over_x(i, g, m, d, part, part, 3).wait_recv()
@@ -277,11 +280,12 @@
         cur = wide(xs[m][piece(g, x), :]) + step * summed(0, g, m)
         inv = lax.rsqrt(jnp.mean(cur * cur, -1, keepdims=True) + EPSILON)
         share(0, g, m, cur * inv * MODS[4 + m : 5 + m, :])
-    share_end(0)
-
-    for h in range(2):
-        make_qkv(T2, lambda m: AG[0, m], h)
-        kv_start(T2, h)
+
+    for m in range(2):
+        share_end(0, m)
+        for h in range(2):
+            make_qkv(T2, AG[0, m], h, m)
+            kv_start(T2, h, m)
     kv_wait(T2, 0)
     for m in range(2):
         attention(T2, m, 0)
@@ -290,6 +294,9 @@
         attention(T2, m, 1)
         SB[1, m] = (ACC[m] - project_out(T2, m)).astype(BF16)
         sum_start(1, m)
+    for m in range(2):
+        for h in range(2):
+            PT[2 * m + h] = PS[2 * m + h].astype(BF16).T
     collect(NG, ng_s, ng_r)
     for s in range(4):
         NGT[128 * s : 128 * s + 128, :] = NG[:, s].reshape(1024, 128).T
@@ -299,38 +306,28 @@
         diff = step * summed(1, g, m)
         DIFF[g, m] = diff
         share(1, g, m, 2.0 * step * diff)
-    share_end(1)
-
-    for m in range(2):
-        DO[m] = dot(AG[1, m], WO[m][...], NT).astype(BF16)
-    for m in range(2):
-        for s in range(16):
-            GS[m, s // 4, s % 4] = AG[1, m, :, 128 * s : 128 * s + 128]
-    GG[v] = GS[core, :, yy]
-    spread(lambda k, y: GS.at[k, :, y], GG, gg_s, gg_r, GG_EARLY)
-
-    def backward(h):
-        for m in range(2):
-            queries = QR[ST, m, :, 128 * h : 128 * h + 128]
-            keys = KV[ST, h, :, :, :, 0:128].reshape(768, 128)
-            values = KV[ST, h, :, :, :, 128:256].reshape(768, 128)
-            grad_out = DO[m, :, 128 * h : 128 * h + 128]
-            prob = PS[2 * m + h]
-            grad_prob = dot(grad_out, values, NT)
-            center = jnp.sum(prob * grad_prob, -1, keepdims=True)
-            dscore = (prob * (grad_prob - center) * factor).astype(BF16)
-            DQ[h, m, :, 0:128] = dot(dscore, keys, NN).astype(BF16)
-            dkey = dot(dscore, queries, TN).reshape(3, 2, 128, 128)
-            dvalue = dot(prob.astype(BF16), grad_out, TN).reshape(3, 2, 128, 128)
-            if m == 0:
-                DKV[h, :, :, :, 0:128] = dkey
-                DKV[h, :, :, :, 128:256] = dvalue
-            else:
-                for slot in (0, 2):
-                    DKS[h, slot // 2, :, :, 0:128] = (DKV[h, slot, :, :, 0:128] + dkey[slot]).astype(BF16)
-                    DKS[h, slot // 2, :, :, 128:256] = (DKV[h, slot, :, :, 128:256] + dvalue[slot]).astype(BF16)
-                DKV[h, 1, :, :, 0:128] = DKV[h, 1, :, :, 0:128] + dkey[1]
-                DKV[h, 1, :, :, 128:256] = DKV[h, 1, :, :, 128:256] + dvalue[1]
+
+    def backward(h, m):
+        queries = QR[ST, m, :, 128 * h : 128 * h + 128]
+        keys = KV[ST, h, :, :, :, 0:128].reshape(768, 128)
+        values = KV[ST, h, :, :, :, 128:256].reshape(768, 128)
+        grad_out = DO[m, :, 128 * h : 128 * h + 128]
+        prob = PS[2 * m + h]
+        grad_prob = dot(grad_out, values, NT)
+        center = jnp.sum(prob * grad_prob, -1, keepdims=True)
+        dscore = (prob * (grad_prob - center) * factor).astype(BF16)
+        DQ[h, m, :, 0:128] = dot(dscore, keys, NN).astype(BF16)
+        dkey = dot(dscore, queries, TN).reshape(3, 2, 128, 128)
+        dvalue = dot(PT[2 * m + h], grad_out, NN).reshape(3, 2, 128, 128)
+        if m == 0:
+            DKV[h, :, :, :, 0:128] = dkey
+            DKV[h, :, :, :, 128:256] = dvalue
+        else:
+            for slot in (0, 2):
+                DKS[h, slot // 2, :, :, 0:128] = (DKV[h, slot, :, :, 0:128] + dkey[slot]).astype(BF16)
+                DKS[h, slot // 2, :, :, 128:256] = (DKV[h, slot, :, :, 128:256] + dvalue[slot]).astype(BF16)
+            DKV[h, 1, :, :, 0:128] = DKV[h, 1, :, :, 0:128] + dkey[1]
+            DKV[h, 1, :, :, 128:256] = DKV[h, 1, :, :, 128:256] + dvalue[1]
 
     def edges(h):
         return [
@@ -364,10 +361,14 @@
         line(n, 2, DG.at[n, y_two], 2 * y_two + core).wait_recv()
         line(n, 3, DG.at[n, y_last], 2 * y_two + core).wait_recv()
 
-    for h in range(2):
-        backward(h)
-        for copy in edges(h):
-            go(copy)
+    for m in range(2):
+        share_end(1, m)
+        DO[m] = dot(AG[1, m], WO[m][...], NT).astype(BF16)
+        for h in range(2):
+            backward(h, m)
+            if m == 1:
+                for copy in edges(h):
+                    go(copy)
     finish_kv(0)
     line_start(0)
     for m in range(2):
@@ -423,17 +424,25 @@
         clip_start(n)
 
     line_on(1)
-    spread(lambda k, y: GS.at[k, :, y], GG, gg_s, gg_r, GG_LATE)
+    for m in range(2):
+        for s in range(16):
+            GS[m, s // 4, s % 4] = AG[1, m, :, 128 * s : 128 * s + 128]
+    GG[v] = GS[core, :, yy]
+    spread(lambda k, y: GS.at[k, :, y], GG, gg_s, gg_r, whole)
     sum_on(2)
     line_grad(0)
+    def back_on(m):
+        for g in range(GROUPS):
+            cur = wide(xs[m][piece(g, x), :])
+            inv = lax.rsqrt(jnp.mean(cur * cur, -1, keepdims=True) + EPSILON)
+            scaled = summed(2, g, m) * MODS[2 + m : 3 + m, :]
+            back = inv * scaled - cur * (inv * inv * inv) * jnp.mean(scaled * cur, -1, keepdims=True)
+            share(2, g, m, DIFF[g, m] + back)
+
+    back_on(0)
     line_grad(1)
     clip_on(0)
-    for g, m in chunks:
-        cur = wide(xs[m][piece(g, x), :])
-        inv = lax.rsqrt(jnp.mean(cur * cur, -1, keepdims=True) + EPSILON)
-        scaled = summed(2, g, m) * MODS[2 + m : 3 + m, :]
-        back = inv * scaled - cur * (inv * inv * inv) * jnp.mean(scaled * cur, -1, keepdims=True)
-        share(2, g, m, DIFF[g, m] + back)
+    back_on(1)
     collect(GG, gg_s, gg_r)
     o_all = OG[...].reshape(1024, 256)
     for s in range(4):
@@ -446,7 +455,8 @@
     for h in range(2):
         for m, total in enumerate(clip_end(h)):
             q_outs[m][:, h, :] = total
-    share_end(2)
+    for m in range(2):
+        share_end(2, m)
     dv_out[...] = AG[2, 0]
     da_out[...] = AG[2, 1]
     for m, total in enumerate(clip_end(2)):
@@ -478,7 +488,7 @@
             vm((8, 4, 128, 128)), vm((512, 1024)), vm((3, 2, 128, 256)), vm((8, 128, 256)),
             vm((2, 4, 4, 128, 128)), vm((8, 4, 128, 128)), vm((2, 2, 128, 384)),
             vm((2, 4, 2, 128, 384)), vm((3, 2, 128, 256)),
-            vm((3, 2, 3, 2, 128, 256)), vm((4, 128, 768), F32), vm((2, 128, 2048), F32),
+            vm((3, 2, 3, 2, 128, 256)), vm((4, 128, 768), F32), vm((4, 768, 128)), vm((2, 128, 2048), F32),
             vm((3, 2, 128, 2048)), vm((3, GROUPS, 2, 3, PIECE, 2048)),
             vm((3, GROUPS, 2, PIECE, 2048)), vm((3, GROUPS, 2, PIECE, 2048)),
             vm((3, 2, 128, 2048)), vm((GROUPS, 2, PIECE, 2048), F32), vm((2, 128, 256)),
@@ -486,7 +496,7 @@
             vm((2, 4, 128, 384)), vm((2, 2, 128, 384)), vm((2, 2, 128, 384)), vm((2, 2, 2, 64, 384)),
             vm((4, 128, 256)), vm((2, 128, 256)), vm((2, 128, 256)), vm((2, 2, 64, 256)),
             vm((8, 2048), F32), vm((2, 128, 768), F32),
-            dma((3, 2, 2)), dma((3, 2, 2)), dma((3, GROUPS, 2, 7)), dma((3, GROUPS, 2, 7)),
+            dma((3, 2, 2, 2)), dma((3, 2, 2, 2)), dma((3, GROUPS, 2, 7)), dma((3, GROUPS, 2, 7)),
             dma((8,)), dma((8,)), dma((8,)), dma((8,)), dma((8,)), dma((8,)),
             dma((2, 2)), dma((2, 2)), dma((2, 4)), dma((2, 4)), dma((3, 5)), dma((3, 2)), dma((3, 2, 2)),
         ],

time: 141 us -> 137 us (0.972)
  Pallas kernels: 135 us -> 132 us
    pallas_call x1, Pallas kernels: 134 us -> 130 us  [fused(): pl.pallas_call(kernel, out_shape=(shape((128, 2048), BF16), shape((128, 2...]
where the time goes in v6:
time: 137 us
  Pallas kernels  132 us (96%)
  local copies, waits for them, and re-layouts  4.95 us (4%)
    pallas_call x1, Pallas kernels, fused(): pl.pallas_call(kernel, out_shape=(shape((128, 2048), BF16), shape((128, 2...  130 us
    unnamed x26, local copies, waits for them, and re-layouts  4.95 us

profile of v6, /device:TPU:1, one launch (start us, length us, event | category | flops | bytes accessed | tf_op | source)
XLA Modules:
  0.0 137.4 jit_solution(11469762777079370979)
XLA Ops:
  0.6 0.0 copy-start.11
  0.6 2.7 %copy.19 = bf16[256,8,2,384]{3,1,2,0:T(8,128)(2,1)S(1)} copy(bf16[256,8,2,384]{3,2,1,0:T(2,128)(2,1)} %bitcast.24) | data formatting | bytes 6291456
  3.3 0.1 copy-done.11
  3.5 0.0 copy-start
  3.5 0.0 copy-start.1
  3.5 0.0 copy-start.2
  3.5 0.0 copy-start.3
  3.5 0.0 copy-start.4
  3.5 0.0 copy-start.5
  3.5 0.0 copy-start.6
  3.5 0.0 copy-start.7
  3.5 0.0 copy-start.8
  3.5 0.0 copy-start.9
  3.6 0.0 copy-start.10
  3.6 0.6 copy.20
  4.2 0.5 copy-done
  4.7 0.3 copy-done.1
  5.0 0.2 copy-done.2
  5.2 0.2 copy-done.3
  5.4 0.2 copy-done.4
  5.5 0.1 copy-done.5
  5.7 0.0 copy-done.6
  5.7 0.0 copy-done.7
  5.7 0.0 copy-done.8
  5.7 0.0 copy-done.9
  5.7 0.0 copy-done.10
  5.7 130.4 %step.1 = (bf16[128,2048]{1,0:T(8,128)(2,1)S(1)}, bf16[128,2048]{1,0:T(8,128)(2,1)S(1)}, f32[64,2,384]{2,1,0:T(2,128)S(1)}, f32[64,2,384]{2,1,0:T(2,128)S(1)}, f...) custom-call(s32[1,2]{1,0:T(1,128)S(1)} %copy-done.9, s32[1,2]{1,0:T(1,128)S(1)} %copy-done.10, ...), custom_call_target="tpu_custom_call" | custom-call | tf_op jit(solution)/shard_map/step/pallas_call | solution.py:478
  136.0 1.2 finish.1
Async XLA Ops:
  0.6 2.8 %copy-start.11 = (bf16[2048,2,384]{2,1,0:T(2,128)(2,1)S(1)}, bf16[2048,2,384]{2,1,0:T(2,128)(2,1)}, u32[]{:S(2)}) copy-start(bf16[2048,2,384]{2,1,0:T(2,128)(2,1)} %param.17) | copy-start | bytes 9437188
  3.5 1.2 copy-start
  3.5 1.5 %copy-start.1 = (bf16[2,128,2048]{2,1,0:T(8,128)(2,1)S(1)}, bf16[2,128,2048]{2,1,0:T(8,128)(2,1)}, u32[]{:S(2)}) copy-start(bf16[2,128,2048]{2,1,0:T(8,128)(2,1)} %param.18) | copy-start | bytes 3145732
  3.5 1.7 %copy-start.2 = (f32[65,2048]{1,0:T(8,128)S(1)}, f32[65,2048]{1,0:T(8,128)}, u32[]{:S(2)}) copy-start(f32[65,2048]{1,0:T(8,128)} %tf.1) | copy-start | bytes 1597444
  3.5 1.9 %copy-start.3 = (f32[65,2048]{1,0:T(8,128)S(1)}, f32[65,2048]{1,0:T(8,128)}, u32[]{:S(2)}) copy-start(f32[65,2048]{1,0:T(8,128)} %tt.1) | copy-start | bytes 1597444
  3.5 2.1 %copy-start.4 = (bf16[1,128,2048]{2,1,0:T(8,128)(2,1)S(1)}, bf16[1,128,2048]{2,1,0:T(8,128)(2,1)}, u32[]{:S(2)}) copy-start(bf16[1,128,2048]{2,1,0:T(8,128)(2,1)} %param.13) | copy-start | bytes 1572868
  3.5 2.2 %copy-start.5 = (bf16[1,128,2048]{2,1,0:T(8,128)(2,1)S(1)}, bf16[1,128,2048]{2,1,0:T(8,128)(2,1)}, u32[]{:S(2)}) copy-start(bf16[1,128,2048]{2,1,0:T(8,128)(2,1)} %param.14) | copy-start | bytes 1572868
  3.5 2.2 %copy-start.6 = (f32[2048]{0:T(1024)S(1)}, f32[2048]{0:T(1024)}, u32[]{:S(2)}) copy-start(f32[2048]{0:T(1024)} %param.19) | copy-start | bytes 24580
  3.5 2.1 %copy-start.7 = (f32[2048]{0:T(1024)S(1)}, f32[2048]{0:T(1024)}, u32[]{:S(2)}) copy-start(f32[2048]{0:T(1024)} %param.20) | copy-start | bytes 24580
  3.5 2.1 %copy-start.8 = (s32[1,32,2]{1,2,0:T(2,128)S(1)}, s32[1,32,2]{1,2,0:T(2,128)}, u32[]{:S(2)}) copy-start(s32[1,32,2]{1,2,0:T(2,128)} %param.25) | copy-start | bytes 772
  3.5 2.1 %copy-start.9 = (s32[1,2]{1,0:T(1,128)S(1)}, s32[1,2]{1,0:T(1,128)}, u32[]{:S(2)}) copy-start(s32[1,2]{1,0:T(1,128)} %steps.1) | copy-start | bytes 28
  3.6 2.1 %copy-start.10 = (s32[1,2]{1,0:T(1,128)S(1)}, s32[1,2]{1,0:T(1,128)}, u32[]{:S(2)}) copy-start(s32[1,2]{1,0:T(1,128)} %windows.1) | copy-start | bytes 28

commit v7 on v6

--- a/solution.py
+++ b/solution.py
@@ -294,6 +294,7 @@
         attention(T2, m, 1)
         SB[1, m] = (ACC[m] - project_out(T2, m)).astype(BF16)
         sum_start(1, m)
+    sum_on(1)
     for m in range(2):
         for h in range(2):
             PT[2 * m + h] = PS[2 * m + h].astype(BF16).T
@@ -301,7 +302,6 @@
     for s in range(4):
         NGT[128 * s : 128 * s + 128, :] = NG[:, s].reshape(1024, 128).T
     collect(OG, og_s, og_r)
-    sum_on(1)
     for g, m in chunks:
         diff = step * summed(1, g, m)
         DIFF[g, m] = diff
@@ -423,13 +423,13 @@
         WA[n] = dot(NGT[...], DG[n].reshape(1024, 384), NN).astype(BF16).reshape(4, 128, 384)
         clip_start(n)
 
+    sum_on(2)
     line_on(1)
     for m in range(2):
         for s in range(16):
             GS[m, s // 4, s % 4] = AG[1, m, :, 128 * s : 128 * s + 128]
     GG[v] = GS[core, :, yy]
     spread(lambda k, y: GS.at[k, :, y], GG, gg_s, gg_r, whole)
-    sum_on(2)
     line_grad(0)
     def back_on(m):
         for g in range(GROUPS):

time: 137 us -> 136 us (level)
  Pallas kernels: 132 us -> 130 us
    pallas_call x1, Pallas kernels: 130 us -> 129 us  [fused(): pl.pallas_call(kernel, out_shape=(shape((128, 2048), BF16), shape((128, 2...]
where the time goes in v7:
time: 136 us
  Pallas kernels  130 us (96%)
  local copies, waits for them, and re-layouts  4.95 us (4%)
    pallas_call x1, Pallas kernels, fused(): pl.pallas_call(kernel, out_shape=(shape((128, 2048), BF16), shape((128, 2...  129 us
    unnamed x26, local copies, waits for them, and re-layouts  4.95 us

profile of v7, /device:TPU:1, one launch (start us, length us, event | category | flops | bytes accessed | tf_op | source)
XLA Modules:
  0.0 135.8 jit_solution(17469018748567201773)
XLA Ops:
  0.6 0.0 copy-start.11
  0.6 2.7 %copy.19 = bf16[256,8,2,384]{3,1,2,0:T(8,128)(2,1)S(1)} copy(bf16[256,8,2,384]{3,2,1,0:T(2,128)(2,1)} %bitcast.24) | data formatting | bytes 6291456
  3.3 0.1 copy-done.11
  3.5 0.0 copy-start
  3.5 0.0 copy-start.1
  3.5 0.0 copy-start.2
  3.5 0.0 copy-start.3
  3.5 0.0 copy-start.4
  3.5 0.0 copy-start.5
  3.5 0.0 copy-start.6
  3.5 0.0 copy-start.7
  3.5 0.0 copy-start.8
  3.5 0.0 copy-start.9
  3.6 0.0 copy-start.10
  3.6 0.6 copy.20
  4.2 0.5 copy-done
  4.7 0.3 copy-done.1
  5.0 0.2 copy-done.2
  5.2 0.2 copy-done.3
  5.4 0.2 copy-done.4
  5.5 0.1 copy-done.5
  5.7 0.0 copy-done.6
  5.7 0.0 copy-done.7
  5.7 0.0 copy-done.8
  5.7 0.0 copy-done.9
  5.7 0.0 copy-done.10
  5.7 128.8 %step.1 = (bf16[128,2048]{1,0:T(8,128)(2,1)S(1)}, bf16[128,2048]{1,0:T(8,128)(2,1)S(1)}, f32[64,2,384]{2,1,0:T(2,128)S(1)}, f32[64,2,384]{2,1,0:T(2,128)S(1)}, f...) custom-call(s32[1,2]{1,0:T(1,128)S(1)} %copy-done.9, s32[1,2]{1,0:T(1,128)S(1)} %copy-done.10, ...), custom_call_target="tpu_custom_call" | custom-call | tf_op jit(solution)/shard_map/step/pallas_call | solution.py:478
  134.5 1.2 finish.1
Async XLA Ops:
  0.6 2.8 %copy-start.11 = (bf16[2048,2,384]{2,1,0:T(2,128)(2,1)S(1)}, bf16[2048,2,384]{2,1,0:T(2,128)(2,1)}, u32[]{:S(2)}) copy-start(bf16[2048,2,384]{2,1,0:T(2,128)(2,1)} %param.17) | copy-start | bytes 9437188
  3.5 1.2 copy-start
  3.5 1.5 %copy-start.1 = (bf16[2,128,2048]{2,1,0:T(8,128)(2,1)S(1)}, bf16[2,128,2048]{2,1,0:T(8,128)(2,1)}, u32[]{:S(2)}) copy-start(bf16[2,128,2048]{2,1,0:T(8,128)(2,1)} %param.18) | copy-start | bytes 3145732
  3.5 1.7 %copy-start.2 = (f32[65,2048]{1,0:T(8,128)S(1)}, f32[65,2048]{1,0:T(8,128)}, u32[]{:S(2)}) copy-start(f32[65,2048]{1,0:T(8,128)} %tf.1) | copy-start | bytes 1597444
  3.5 1.9 %copy-start.3 = (f32[65,2048]{1,0:T(8,128)S(1)}, f32[65,2048]{1,0:T(8,128)}, u32[]{:S(2)}) copy-start(f32[65,2048]{1,0:T(8,128)} %tt.1) | copy-start | bytes 1597444
  3.5 2.1 %copy-start.4 = (bf16[1,128,2048]{2,1,0:T(8,128)(2,1)S(1)}, bf16[1,128,2048]{2,1,0:T(8,128)(2,1)}, u32[]{:S(2)}) copy-start(bf16[1,128,2048]{2,1,0:T(8,128)(2,1)} %param.13) | copy-start | bytes 1572868
  3.5 2.2 %copy-start.5 = (bf16[1,128,2048]{2,1,0:T(8,128)(2,1)S(1)}, bf16[1,128,2048]{2,1,0:T(8,128)(2,1)}, u32[]{:S(2)}) copy-start(bf16[1,128,2048]{2,1,0:T(8,128)(2,1)} %param.14) | copy-start | bytes 1572868
  3.5 2.2 %copy-start.6 = (f32[2048]{0:T(1024)S(1)}, f32[2048]{0:T(1024)}, u32[]{:S(2)}) copy-start(f32[2048]{0:T(1024)} %param.19) | copy-start | bytes 24580
  3.5 2.1 %copy-start.7 = (f32[2048]{0:T(1024)S(1)}, f32[2048]{0:T(1024)}, u32[]{:S(2)}) copy-start(f32[2048]{0:T(1024)} %param.20) | copy-start | bytes 24580
  3.5 2.1 %copy-start.8 = (s32[1,32,2]{1,2,0:T(2,128)S(1)}, s32[1,32,2]{1,2,0:T(2,128)}, u32[]{:S(2)}) copy-start(s32[1,32,2]{1,2,0:T(2,128)} %param.25) | copy-start | bytes 772
  3.5 2.1 %copy-start.9 = (s32[1,2]{1,0:T(1,128)S(1)}, s32[1,2]{1,0:T(1,128)}, u32[]{:S(2)}) copy-start(s32[1,2]{1,0:T(1,128)} %steps.1) | copy-start | bytes 28
  3.6 2.1 %copy-start.10 = (s32[1,2]{1,0:T(1,128)S(1)}, s32[1,2]{1,0:T(1,128)}, u32[]{:S(2)}) copy-start(s32[1,2]{1,0:T(1,128)} %windows.1) | copy-start | bytes 28
